TPU v7x, 32 devices: a whole 2x2x4 slice. The times are simulated.
32 devices in a mesh: head: 2 (over y), ctx: 16 (over z, x, core).
Axes of the slice: x: 2, y: 2, z: 4, core: 2. Of those that a mesh axis runs over, the one named last changes fastest.
Arguments:
- video_q: bfloat16 [4096, 2048], P('ctx', 'head'), may hold values from -8 to 8
- video_k: bfloat16 [4096, 2048], P('ctx', 'head'), may hold values from -8 to 8
- video_v: bfloat16 [4096, 2048], P('ctx', 'head'), may hold values from -6 to 6
- audio_q: bfloat16 [128, 2048], P('ctx', 'head'), may hold values from -8 to 8
- audio_k: bfloat16 [128, 2048], P('ctx', 'head'), may hold values from -8 to 8
- audio_v: bfloat16 [128, 2048], P('ctx', 'head'), may hold values from -6 to 6
- video_length: int32 [1], replicated, may hold values from 2048 to 4096
- video_cot: bfloat16 [16, 256, 2048], P('ctx', 'head'), may hold values from -6 to 6
- audio_cot: bfloat16 [128, 2048], P('ctx', 'head'), may hold values from -6 to 6
Outputs:
- video_out: bfloat16 [16, 256, 2048], P('ctx', 'head')
- audio_out: bfloat16 [128, 2048], P('ctx', 'head')
- grad_video_q: bfloat16 [4096, 2048], P('ctx', 'head')
- grad_video_k: bfloat16 [4096, 2048], P('ctx', 'head')
- grad_video_v: bfloat16 [4096, 2048], P('ctx', 'head')
- grad_audio_q: bfloat16 [128, 2048], P('ctx', 'head')
- grad_audio_k: bfloat16 [128, 2048], P('ctx', 'head')
- grad_audio_v: bfloat16 [128, 2048], P('ctx', 'head')
All inputs are finite; a program needn't handle non-finite values.
Results may differ from a plain program's by a relative error of at most 0.011.
Values may be sent and summed in bfloat16 or wider, within the bound.
No kernel may reach another device: no remote copies, remote signals or barrier semaphores. Data moves between devices by JAX's collectives and lax.ppermute only.
A program may use at most 64 MiB of HBM per device.

v0:
```python
import jax
import jax.numpy as jnp
from jax import lax
from jax.sharding import PartitionSpec as P

HEAD_DIM = 64


def head_slice(matrix, head_num):
    return matrix[:, head_num * HEAD_DIM : (head_num + 1) * HEAD_DIM]


def head_sums(matrix, local_heads):
    return matrix.reshape(matrix.shape[0], local_heads, HEAD_DIM).sum(axis=2)


def expand_heads(per_head):
    return jnp.repeat(per_head, HEAD_DIM, axis=1)


def body(video_q, video_k, video_v, audio_q, audio_k, audio_v, video_length, video_cot, audio_cot):
    score_scale = HEAD_DIM ** (-0.5)
    vid_rows, feat_width = video_q.shape
    local_heads = feat_width // HEAD_DIM
    aud_rows = audio_q.shape[0]
    ctx_index = lax.axis_index("ctx")
    audio_keys, audio_values = (
        lax.all_gather(audio_k, "ctx", axis=0, tiled=True),
        lax.all_gather(audio_v, "ctx", axis=0, tiled=True),
    )
    audio_queries = lax.all_gather(audio_q, "ctx", axis=0, tiled=True)
    token_index = ctx_index * vid_rows + lax.iota(jnp.int32, vid_rows)
    is_live = (token_index < video_length[0])[None, :]
    cross_scores = []
    local_max = []
    for head_num in range(local_heads):
        scores = (
            jnp.einsum(
                "ad,vd->av",
                head_slice(audio_queries, head_num),
                head_slice(video_k, head_num),
                preferred_element_type=jnp.float32,
            )
            * score_scale
        )
        cross_scores.append(scores)
        local_max.append(jnp.max(jnp.where(is_live, scores, -1e30), axis=1))
    global_max = lax.pmax(jnp.stack(local_max, axis=1), "ctx")
    video_probs = []
    video_bprobs = []
    video_parts = []
    for head_num in range(local_heads):
        scores = (
            jnp.einsum(
                "vd,ad->va",
                head_slice(video_q, head_num),
                head_slice(audio_keys, head_num),
                preferred_element_type=jnp.float32,
            )
            * score_scale
        )
        shifted = jnp.exp(scores - jnp.max(scores, axis=1, keepdims=True))
        probs = shifted / jnp.sum(shifted, axis=1, keepdims=True)
        rounded = probs.astype(jnp.bfloat16)
        video_probs.append(probs)
        video_bprobs.append(rounded)
        video_parts.append(
            jnp.einsum(
                "va,ad->vd",
                rounded,
                head_slice(audio_values, head_num),
                preferred_element_type=jnp.float32,
            )
        )
    video_attended = jnp.concatenate(video_parts, axis=1)
    video_out = lax.all_to_all(
        video_attended.astype(jnp.bfloat16), "head", split_axis=0, concat_axis=1, tiled=True
    )[None]
    audio_weights = []
    numer_parts = []
    total_parts = []
    for head_num in range(local_heads):
        weights = jnp.where(
            is_live, jnp.exp(cross_scores[head_num] - global_max[:, head_num : head_num + 1]), 0.0
        )
        audio_weights.append(weights)
        numer_parts.append(
            jnp.einsum(
                "av,vd->ad",
                weights.astype(jnp.bfloat16),
                head_slice(video_v, head_num),
                preferred_element_type=jnp.float32,
            )
        )
        total_parts.append(jnp.sum(weights, axis=1))
    numerators = jnp.concatenate(numer_parts, axis=1)
    totals = jnp.stack(total_parts, axis=1)
    audio_grads_all = lax.all_gather(audio_cot, "ctx", axis=0, tiled=True)
    numer_all, totals_all = lax.psum((numerators, totals), "ctx")
    audio_attended = numer_all / expand_heads(totals_all)
    projected = head_sums(audio_grads_all.astype(jnp.float32) * audio_attended, local_heads)
    audio_out = lax.dynamic_slice_in_dim(audio_attended, ctx_index * aud_rows, aud_rows, 0).astype(
        jnp.bfloat16
    )
    video_grad = lax.all_to_all(video_cot[0], "head", split_axis=1, concat_axis=0, tiled=True)
    video_proj = head_sums(video_grad.astype(jnp.float32) * video_attended, local_heads)
    video_steps = []
    video_q_grads = []
    for head_num in range(local_heads):
        dprob = jnp.einsum(
            "vd,ad->va",
            head_slice(video_grad, head_num),
            head_slice(audio_values, head_num),
            preferred_element_type=jnp.float32,
        )
        dscore = (
            score_scale * video_probs[head_num] * (dprob - video_proj[:, head_num : head_num + 1])
        ).astype(jnp.bfloat16)
        video_steps.append(dscore)
        video_q_grads.append(
            jnp.einsum(
                "va,ad->vd",
                dscore,
                head_slice(audio_keys, head_num),
                preferred_element_type=jnp.float32,
            )
        )
    audio_steps = []
    video_k_grads = []
    video_v_grads = []
    for head_num in range(local_heads):
        probs = audio_weights[head_num] / totals_all[:, head_num : head_num + 1]
        dprob = jnp.einsum(
            "ad,vd->av",
            head_slice(audio_grads_all, head_num),
            head_slice(video_v, head_num),
            preferred_element_type=jnp.float32,
        )
        dscore = (score_scale * probs * (dprob - projected[:, head_num : head_num + 1])).astype(
            jnp.bfloat16
        )
        audio_steps.append(dscore)
        video_k_grads.append(
            jnp.einsum(
                "av,ad->vd",
                dscore,
                head_slice(audio_queries, head_num),
                preferred_element_type=jnp.float32,
            )
        )
        video_v_grads.append(
            jnp.einsum(
                "av,ad->vd",
                probs.astype(jnp.bfloat16),
                head_slice(audio_grads_all, head_num),
                preferred_element_type=jnp.float32,
            )
        )
    step_stack = jnp.stack(video_steps)
    prob_stack = jnp.stack(video_bprobs)
    audio_stack = jnp.stack(audio_steps)
    queries_split = video_q.reshape(vid_rows, local_heads, HEAD_DIM)
    grads_split = video_grad.reshape(vid_rows, local_heads, HEAD_DIM)
    keys_split = video_k.reshape(vid_rows, local_heads, HEAD_DIM)
    step_part = step_stack
    key_grad = jnp.einsum(
        "hva,vhd->ahd", step_part, queries_split, preferred_element_type=jnp.float32
    ).reshape(aud_rows * lax.axis_size("ctx"), feat_width)
    value_grad = jnp.einsum(
        "hva,vhd->ahd", prob_stack, grads_split, preferred_element_type=jnp.float32
    ).reshape(aud_rows * lax.axis_size("ctx"), feat_width)
    step_part = audio_stack
    combined = lax.psum_scatter(
        jnp.concatenate(
            [
                jnp.concatenate([key_grad, value_grad], axis=1),
                jnp.einsum(
                    "hav,vhd->ahd", step_part, keys_split, preferred_element_type=jnp.float32
                ).reshape(aud_rows * lax.axis_size("ctx"), feat_width),
            ],
            axis=1,
        ),
        "ctx",
        scatter_dimension=0,
        tiled=True,
    )
    key_sums = combined[:, : 2 * feat_width]
    query_sums = combined[:, 2 * feat_width :]
    grad_video_q = jnp.concatenate(video_q_grads, axis=1).astype(jnp.bfloat16)
    grad_video_k = jnp.concatenate(video_k_grads, axis=1).astype(jnp.bfloat16)
    grad_video_v = jnp.concatenate(video_v_grads, axis=1).astype(jnp.bfloat16)
    grad_audio_q = query_sums.astype(jnp.bfloat16)
    grad_audio_k = key_sums[:, :feat_width].astype(jnp.bfloat16)
    grad_audio_v = key_sums[:, feat_width:].astype(jnp.bfloat16)
    return (
        video_out,
        audio_out,
        grad_video_q,
        grad_video_k,
        grad_video_v,
        grad_audio_q,
        grad_audio_k,
        grad_audio_v,
    )


def solution(mesh):
    return jax.shard_map(
        body,
        mesh=mesh,
        in_specs=(
            P("ctx", "head"),
            P("ctx", "head"),
            P("ctx", "head"),
            P("ctx", "head"),
            P("ctx", "head"),
            P("ctx", "head"),
            P(),
            P("ctx", "head", None),
            P("ctx", "head"),
        ),
        out_specs=(
            P("ctx", "head", None),
            P("ctx", "head"),
            P("ctx", "head"),
            P("ctx", "head"),
            P("ctx", "head"),
            P("ctx", "head"),
            P("ctx", "head"),
            P("ctx", "head"),
        ),
        check_vma=False,
    )
```

profile of v0, /device:TPU:0, one launch (start us, length us, event | category | flops | bytes accessed | tf_op | source)
XLA Modules:
  0.0 371.4 jit_solution(5722684182839939890)
XLA Ops:
  7.2 24.2 %all_gather.14 = bf16[128,1024]{1,0:T(8,128)(2,1)S(1)} all-gather(bf16[8,1024]{1,0:T(8,128)(2,1)} %param.12), channel_id=1, replica_groups=mesh['head'=2,'ctx'=16] {'ctx'}, dimensions={0}, use_global_device_ids=true | all-gather | bytes 278528 | tf_op jit(solution)/shard_map/all_gather | solution.py:31
  31.4 1.0 convolution_multiply_fusion.1
  32.4 1.1 convolution_multiply_fusion.2
  33.6 1.1 convolution_multiply_fusion.3
  34.6 1.1 convolution_multiply_fusion.4
  35.8 1.1 convolution_multiply_fusion.5
  36.9 1.1 convolution_multiply_fusion.6
  41.1 30.3 %pmax.7 = f32[128,16]{0,1:T(8,128)S(1)} all-reduce(f32[128,16]{0,1:T(8,128)S(1)} %stack.271), channel_id=1, replica_groups=mesh['head'=2,'ctx'=16] {'ctx'}, use_global_device_ids=true, to_apply=%region_48.49 | all-reduce | flops 2048 | bytes 16384 | tf_op jit(solution)/shard_map/pmax | solution.py:48
  85.6 2.0 copy.140
  87.7 3.6 all-to-all-start.1
  91.3 2.1 fusion.187
  93.5 2.0 fusion.190
  95.5 18.1 %all_gather.12 = bf16[128,1024]{1,0:T(8,128)(2,1)S(1)} all-gather(bf16[8,1024]{1,0:T(8,128)(2,1)S(1)} %copy-done.104), channel_id=1, replica_groups=mesh['head'=2,'ctx'=16] {'ctx'}, dimensions={0}, use_global_device_ids=true | all-gather | bytes 278528 | tf_op jit(solution)/shard_map/all_gather | solution.py:28
  114.4 1.4 fusion.576
  115.8 1.5 fusion.575
  117.3 1.4 fusion.574
  118.8 1.5 fusion.573
  120.3 1.4 fusion.572
  121.7 1.5 fusion.571
  123.2 1.3 fusion.570
  124.5 1.4 fusion.569
  125.9 1.3 fusion.568
  127.2 1.4 fusion.567
  128.7 1.4 fusion.566
  130.0 1.5 fusion.565
  131.5 1.4 fusion.564
  132.9 1.5 fusion.563
  134.4 1.4 fusion.562
  135.7 21.3 %all_gather.15 = bf16[128,1024]{1,0:T(8,128)(2,1)} all-gather(bf16[8,1024]{1,0:T(8,128)(2,1)S(1)} %copy-done.105), channel_id=1, replica_groups=mesh['head'=2,'ctx'=16] {'ctx'}, dimensions={0}, use_global_device_ids=true | all-gather | bytes 278528 | tf_op jit(solution)/shard_map/all_gather | solution.py:98
  157.2 30.5 %psum.15 = f32[128,16]{0,1:T(8,128)S(1)} all-reduce(f32[128,16]{0,1:T(8,128)S(1)} %stack.288), channel_id=1, replica_groups=mesh['head'=2,'ctx'=16] {'ctx'}, use_global_device_ids=true, to_apply=%region_66.67 | all-reduce | flops 2048 | bytes 16384 | tf_op jit(solution)/shard_map/psum | solution.py:99
  187.9 18.3 %all_gather.13 = bf16[128,1024]{1,0:T(8,128)(2,1)S(1)} all-gather(bf16[8,1024]{1,0:T(8,128)(2,1)} %param.14), channel_id=1, replica_groups=mesh['head'=2,'ctx'=16] {'ctx'}, dimensions={0}, use_global_device_ids=true | all-gather | bytes 278528 | tf_op jit(solution)/shard_map/all_gather | solution.py:29
  224.0 1.1 fusion.79
  231.3 1.0 constant_dynamic-update-slice_fusion.30
  252.9 1.8 copy.159
  254.7 1.0 copy.160
  255.7 1.0 copy.163
  256.7 2.0 copy.171
  259.3 1.8 bitcast_reduce_fusion
  261.8 4.4 %all-to-all-start = ((bf16[2,128,1024]{1,2,0:T(8,128)(2,1)}), bf16[2,128,1024]{1,2,0:T(8,128)(2,1)}, u32[]{:S(2)}, u32[]{:S(2)}) async-start(bf16[2,128,1024]{1,2,0:T(8,128)(2,1)} %constant_dynamic-update-slice_fusion), calls=%async_computation | async-start | bytes 1048576 | tf_op jit(solution)/shard_map/all_to_all | solution.py:76
  266.5 1.3 copy.142
  267.8 1.4 all_to_all.32
  270.3 1.6 constant_dynamic-update-slice_fusion.78
  285.6 1.7 fusion.579
  287.5 1.4 multiply_reduce_fusion
  289.3 1.5 constant_dynamic-update-slice_fusion.47
  302.6 1.2 pad_maximum_fusion
  311.9 2.1 copy.167
  317.3 45.7 %reduce-scatter.2.cloned.1.call-done = f32[8,3072]{1,0:T(8,128)} async-done(((f32[128,3072]{1,0:T(8,128)}), f32[8,3072]{1,0:T(8,128)}) %reduce-scatter.2.cloned.1.call-update) | async-done | bytes 98320 | tf_op jit(solution)/shard_map/reduce_scatter | solution.py:173
  (725 shorter events, 100.7 us)
Async XLA Ops:
  7.2 252.2 %all-reduce.2.cloned.1.call-start = ((), (), s32[]{:S(2)}) async-start(), calls=%async_computation.3 | async-start | bytes 1048576 | tf_op jit(solution)/shard_map/psum | solution.py:99
  32.4 58.9 %copy-start.11 = (f32[128,256]{1,0:T(8,128)}, f32[128,256]{1,0:T(8,128)S(1)}, u32[]{:S(2)}) copy-start(f32[128,256]{1,0:T(8,128)S(1)} %convolution_multiply_fusion.1) | copy-start | bytes 393220
  33.6 49.3 %copy-start.14 = (f32[128,256]{1,0:T(8,128)}, f32[128,256]{1,0:T(8,128)S(1)}, u32[]{:S(2)}) copy-start(f32[128,256]{1,0:T(8,128)S(1)} %convolution_multiply_fusion.2) | copy-start | bytes 393220
  34.6 47.4 %copy-start.17 = (f32[128,256]{1,0:T(8,128)}, f32[128,256]{1,0:T(8,128)S(1)}, u32[]{:S(2)}) copy-start(f32[128,256]{1,0:T(8,128)S(1)} %convolution_multiply_fusion.3) | copy-start | bytes 393220
  35.8 45.4 %copy-start.20 = (f32[128,256]{1,0:T(8,128)}, f32[128,256]{1,0:T(8,128)S(1)}, u32[]{:S(2)}) copy-start(f32[128,256]{1,0:T(8,128)S(1)} %convolution_multiply_fusion.4) | copy-start | bytes 393220
  36.8 43.4 %copy-start.23 = (f32[128,256]{1,0:T(8,128)}, f32[128,256]{1,0:T(8,128)S(1)}, u32[]{:S(2)}) copy-start(f32[128,256]{1,0:T(8,128)S(1)} %convolution_multiply_fusion.5) | copy-start | bytes 393220
  38.0 41.4 %copy-start.26 = (f32[128,256]{1,0:T(8,128)}, f32[128,256]{1,0:T(8,128)S(1)}, u32[]{:S(2)}) copy-start(f32[128,256]{1,0:T(8,128)S(1)} %convolution_multiply_fusion.6) | copy-start | bytes 393220
  38.2 40.4 %copy-start.29 = (f32[128,256]{1,0:T(8,128)}, f32[128,256]{1,0:T(8,128)S(1)}, u32[]{:S(2)}) copy-start(f32[128,256]{1,0:T(8,128)S(1)} %convolution_multiply_fusion.7) | copy-start | bytes 393220
  39.5 54.0 %copy-start.3 = (f32[128,256]{1,0:T(8,128)}, f32[128,256]{1,0:T(8,128)S(1)}, u32[]{:S(2)}) copy-start(f32[128,256]{1,0:T(8,128)S(1)} %convolution_multiply_fusion.13) | copy-start | bytes 393220
  39.7 53.7 %copy-start.6 = (f32[128,256]{1,0:T(8,128)}, f32[128,256]{1,0:T(8,128)S(1)}, u32[]{:S(2)}) copy-start(f32[128,256]{1,0:T(8,128)S(1)} %convolution_multiply_fusion.14) | copy-start | bytes 393220
  39.9 53.6 %copy-start.9 = (f32[128,256]{1,0:T(8,128)}, f32[128,256]{1,0:T(8,128)S(1)}, u32[]{:S(2)}) copy-start(f32[128,256]{1,0:T(8,128)S(1)} %convolution_multiply_fusion.15) | copy-start | bytes 393220
  41.0 43.7 %copy-start.35 = (f32[128,256]{1,0:T(8,128)}, f32[128,256]{1,0:T(8,128)S(1)}, u32[]{:S(2)}) copy-start(f32[128,256]{1,0:T(8,128)S(1)} %get-tuple-element.205) | copy-start | bytes 393220
  87.7 174.1 %all-to-all-start.1 = ((bf16[128,2,1024]{0,2,1:T(8,128)(2,1)}), bf16[128,2,1024]{0,2,1:T(8,128)(2,1)S(1)}, u32[]{:S(2)}, u32[]{:S(2)}) async-start(bf16[128,2,1024]{0,2,1:T(8,128)(2,1)} %bitcast.467), calls=%async_computation.1 | async-start | bytes 1048576 | tf_op jit(solution)/shard_map/all_to_all | solution.py:105
  118.7 38.3 %copy-start.212 = (f32[128]{0:T(128)S(1)}, f32[128]{0:T(128)}, u32[]{:S(2)}) copy-start(f32[128]{0:T(128)} %get-tuple-element.40) | copy-start | bytes 1540
  118.7 38.3 %copy-start.213 = (f32[128]{0:T(128)S(1)}, f32[128]{0:T(128)}, u32[]{:S(2)}) copy-start(f32[128]{0:T(128)} %get-tuple-element.41) | copy-start | bytes 1540
  118.7 38.3 %copy-start.214 = (f32[128]{0:T(128)S(1)}, f32[128]{0:T(128)}, u32[]{:S(2)}) copy-start(f32[128]{0:T(128)} %get-tuple-element.42) | copy-start | bytes 1540
  118.7 38.3 %copy-start.215 = (f32[128]{0:T(128)S(1)}, f32[128]{0:T(128)}, u32[]{:S(2)}) copy-start(f32[128]{0:T(128)} %get-tuple-element.43) | copy-start | bytes 1540
  118.7 38.3 %copy-start.216 = (f32[128]{0:T(128)S(1)}, f32[128]{0:T(128)}, u32[]{:S(2)}) copy-start(f32[128]{0:T(128)} %get-tuple-element.44) | copy-start | bytes 1540
  118.7 38.3 %copy-start.217 = (f32[128]{0:T(128)S(1)}, f32[128]{0:T(128)}, u32[]{:S(2)}) copy-start(f32[128]{0:T(128)} %get-tuple-element.45) | copy-start | bytes 1540
  118.7 38.3 %copy-start.218 = (f32[128]{0:T(128)S(1)}, f32[128]{0:T(128)}, u32[]{:S(2)}) copy-start(f32[128]{0:T(128)} %get-tuple-element.46) | copy-start | bytes 1540
  118.7 38.3 %copy-start.219 = (f32[128]{0:T(128)S(1)}, f32[128]{0:T(128)}, u32[]{:S(2)}) copy-start(f32[128]{0:T(128)} %get-tuple-element.47) | copy-start | bytes 1540
  118.7 38.3 %copy-start.220 = (f32[128]{0:T(128)S(1)}, f32[128]{0:T(128)}, u32[]{:S(2)}) copy-start(f32[128]{0:T(128)} %get-tuple-element.48) | copy-start | bytes 1540
  118.7 38.3 %copy-start.221 = (f32[128]{0:T(128)S(1)}, f32[128]{0:T(128)}, u32[]{:S(2)}) copy-start(f32[128]{0:T(128)} %get-tuple-element.49) | copy-start | bytes 1540
  118.7 38.3 %copy-start.222 = (f32[128]{0:T(128)S(1)}, f32[128]{0:T(128)}, u32[]{:S(2)}) copy-start(f32[128]{0:T(128)} %get-tuple-element.50) | copy-start | bytes 1540
  118.8 38.3 %copy-start.223 = (f32[128]{0:T(128)S(1)}, f32[128]{0:T(128)}, u32[]{:S(2)}) copy-start(f32[128]{0:T(128)} %get-tuple-element.51) | copy-start | bytes 1540
  118.8 38.3 %copy-start.224 = (f32[128]{0:T(128)S(1)}, f32[128]{0:T(128)}, u32[]{:S(2)}) copy-start(f32[128]{0:T(128)} %get-tuple-element.52) | copy-start | bytes 1540
  118.8 38.3 %copy-start.225 = (f32[128]{0:T(128)S(1)}, f32[128]{0:T(128)}, u32[]{:S(2)}) copy-start(f32[128]{0:T(128)} %get-tuple-element.53) | copy-start | bytes 1540
  118.8 38.3 %copy-start.226 = (f32[128]{0:T(128)S(1)}, f32[128]{0:T(128)}, u32[]{:S(2)}) copy-start(f32[128]{0:T(128)} %get-tuple-element.54) | copy-start | bytes 1540
  118.8 38.3 %copy-start.227 = (f32[128]{0:T(128)S(1)}, f32[128]{0:T(128)}, u32[]{:S(2)}) copy-start(f32[128]{0:T(128)} %get-tuple-element.55) | copy-start | bytes 1540
  187.7 36.3 %copy-start.69 = (bf16[128,1024]{1,0:T(8,128)(2,1)S(1)}, bf16[128,1024]{1,0:T(8,128)(2,1)}, u32[]{:S(2)}) copy-start(bf16[128,1024]{1,0:T(8,128)(2,1)} %all_gather.15) | copy-start | bytes 786436
  187.7 37.5 %copy-start.258 = (f32[128]{0:T(128)}, f32[128]{0:T(128)S(1)}, u32[]{:S(2)}) copy-start(f32[128]{0:T(128)S(1)} %get-tuple-element.140) | copy-start | bytes 1540
  187.7 37.5 %copy-start.256 = (f32[128]{0:T(128)}, f32[128]{0:T(128)S(1)}, u32[]{:S(2)}) copy-start(f32[128]{0:T(128)S(1)} %get-tuple-element.139) | copy-start | bytes 1540
  187.8 37.8 %copy-start.254 = (f32[128]{0:T(128)}, f32[128]{0:T(128)S(1)}, u32[]{:S(2)}) copy-start(f32[128]{0:T(128)S(1)} %get-tuple-element.138) | copy-start | bytes 1540
  187.8 38.0 %copy-start.252 = (f32[128]{0:T(128)}, f32[128]{0:T(128)S(1)}, u32[]{:S(2)}) copy-start(f32[128]{0:T(128)S(1)} %get-tuple-element.137) | copy-start | bytes 1540
  187.8 38.3 %copy-start.250 = (f32[128]{0:T(128)}, f32[128]{0:T(128)S(1)}, u32[]{:S(2)}) copy-start(f32[128]{0:T(128)S(1)} %get-tuple-element.136) | copy-start | bytes 1540
  187.8 38.6 %copy-start.248 = (f32[128]{0:T(128)}, f32[128]{0:T(128)S(1)}, u32[]{:S(2)}) copy-start(f32[128]{0:T(128)S(1)} %get-tuple-element.135) | copy-start | bytes 1540
  187.8 38.9 %copy-start.246 = (f32[128]{0:T(128)}, f32[128]{0:T(128)S(1)}, u32[]{:S(2)}) copy-start(f32[128]{0:T(128)S(1)} %get-tuple-element.134) | copy-start | bytes 1540
  187.8 39.2 %copy-start.244 = (f32[128]{0:T(128)}, f32[128]{0:T(128)S(1)}, u32[]{:S(2)}) copy-start(f32[128]{0:T(128)S(1)} %get-tuple-element.133) | copy-start | bytes 1540
  187.8 39.5 %copy-start.242 = (f32[128]{0:T(128)}, f32[128]{0:T(128)S(1)}, u32[]{:S(2)}) copy-start(f32[128]{0:T(128)S(1)} %get-tuple-element.132) | copy-start | bytes 1540
  187.8 39.8 %copy-start.240 = (f32[128]{0:T(128)}, f32[128]{0:T(128)S(1)}, u32[]{:S(2)}) copy-start(f32[128]{0:T(128)S(1)} %get-tuple-element.131) | copy-start | bytes 1540
  187.8 40.1 %copy-start.238 = (f32[128]{0:T(128)}, f32[128]{0:T(128)S(1)}, u32[]{:S(2)}) copy-start(f32[128]{0:T(128)S(1)} %get-tuple-element.130) | copy-start | bytes 1540
  187.8 40.4 %copy-start.236 = (f32[128]{0:T(128)}, f32[128]{0:T(128)S(1)}, u32[]{:S(2)}) copy-start(f32[128]{0:T(128)S(1)} %get-tuple-element.129) | copy-start | bytes 1540
  187.9 40.7 %copy-start.234 = (f32[128]{0:T(128)}, f32[128]{0:T(128)S(1)}, u32[]{:S(2)}) copy-start(f32[128]{0:T(128)S(1)} %get-tuple-element.128) | copy-start | bytes 1540
  187.9 41.1 %copy-start.232 = (f32[128]{0:T(128)}, f32[128]{0:T(128)S(1)}, u32[]{:S(2)}) copy-start(f32[128]{0:T(128)S(1)} %get-tuple-element.127) | copy-start | bytes 1540
  187.9 41.4 %copy-start.230 = (f32[128]{0:T(128)}, f32[128]{0:T(128)S(1)}, u32[]{:S(2)}) copy-start(f32[128]{0:T(128)S(1)} %get-tuple-element.126) | copy-start | bytes 1540
  187.9 41.7 %copy-start.228 = (f32[128]{0:T(128)}, f32[128]{0:T(128)S(1)}, u32[]{:S(2)}) copy-start(f32[128]{0:T(128)S(1)} %get-tuple-element.125) | copy-start | bytes 1540
  261.8 50.0 %all-to-all-start = ((bf16[2,128,1024]{1,2,0:T(8,128)(2,1)}), bf16[2,128,1024]{1,2,0:T(8,128)(2,1)}, u32[]{:S(2)}, u32[]{:S(2)}) async-start(bf16[2,128,1024]{1,2,0:T(8,128)(2,1)} %constant_dynamic-update-slice_fusion), calls=%async_computation | async-start | bytes 1048576 | tf_op jit(solution)/shard_map/all_to_all | solution.py:76
  266.2 96.9 %reduce-scatter.2.cloned.1.call-start = ((), (), s32[]{:S(2)}) async-start(), calls=%async_computation.4 | async-start | bytes 1671168 | tf_op jit(solution)/shard_map/reduce_scatter | solution.py:173
  (222 other events, 1162.2 us)
Sparse Core Ops, SparseCore 0:
  85.7 88.2 all-reduce.1
  304.2 58.8 reduce-scatter.1
where the time goes:
time: 373 us; the launch traced here: 371 us
  blocking collectives  143 us (38%)
  matrix products  101 us (27%)
  waiting for transfers between devices  45.8 us (12%)
  local copies, waits for them, and re-layouts  29.6 us (8%)
  other arithmetic  26.2 us (7%)
  between operations  18.3 us (5%)
  starting transfers between devices  8.28 us (2%)
    reduce_scatter x1, waiting for transfers between devices, body(): lax.psum_scatter(jnp.concatenate([jnp.concatenate([key_grad, value_grad],...  45.7 us
    psum x1, blocking collectives, body(): numer_all, totals_all = lax.psum((numerators, totals), 'ctx')  30.5 us
    pmax x1, blocking collectives, body(): global_max = lax.pmax(jnp.stack(local_max, axis=1), 'ctx')  30.3 us
    all_gather x1, blocking collectives, body(): audio_queries = lax.all_gather(audio_q, 'ctx', axis=0, tiled=True)  24.2 us
    unnamed x555, local copies, waits for them, and re-layouts  22.2 us
    dot_general x16, matrix products, body(): jnp.einsum('vd,ad->va', head_slice(video_q, head_num), head_slice(audio_k...  22.1 us
    all_gather x1, blocking collectives, body(): audio_grads_all = lax.all_gather(audio_cot, 'ctx', axis=0, tiled=True)  21.3 us
    all_gather x1, blocking collectives, body(): lax.all_gather(audio_v, 'ctx', axis=0, tiled=True)  18.3 us
  transfers between devices with their start and end apart: 4, of which 1 were waited for; matrix products, arithmetic and copies ran while one was open for 35% of the time, Pallas kernels for 0%

commit v1 on v0

v1 whole, which is shorter than its diff:
```python
import functools

import jax
import jax.numpy as jnp
from jax import lax
from jax.experimental import pallas as pl
from jax.experimental.pallas import tpu as pltpu
from jax.sharding import PartitionSpec as P

HEAD_DIM = 64
PAIR = 2 * HEAD_DIM
SCALE = HEAD_DIM ** (-0.5)
NEG = -1e30
F32 = jnp.float32
BF16 = jnp.bfloat16


def nt(x, y):
    return lax.dot_general(x, y, (((1,), (1,)), ((), ())), preferred_element_type=F32)


def nn(x, y):
    return jnp.dot(x, y, preferred_element_type=F32)


def tn(x, y):
    return lax.dot_general(x, y, (((0,), (0,)), ((), ())), preferred_element_type=F32)


def first_head(shape):
    return lax.broadcasted_iota(jnp.int32, shape, len(shape) - 1) < HEAD_DIM


def block_diag(low, high):
    rows = jnp.concatenate([low, high], axis=0)
    keep = first_head(rows.shape)
    zero = jnp.zeros_like(rows)
    return jnp.concatenate([jnp.where(keep, rows, zero), jnp.where(keep, zero, rows)], axis=0)


def join_pair(stacked):
    rows = stacked.shape[0] // 2
    return jnp.where(first_head((rows, PAIR)), stacked[:rows], stacked[rows:])


def audio_kernel(live_ref, q_lo, q_hi, c_lo, c_hi, key_ref, val_ref, stat_ref, keep_ref, send_ref):
    keys, vals = key_ref[...], val_ref[...]
    queries = block_diag(q_lo[...], q_hi[...])
    cots = block_diag(c_lo[...], c_hi[...])
    rows = queries.shape[0] // 2
    scores = nt(queries, keys) * SCALE
    live = lax.broadcasted_iota(jnp.int32, scores.shape, 1) < live_ref[0]
    top = jnp.max(jnp.where(live, scores, NEG), axis=1, keepdims=True)
    weights = jnp.where(live, jnp.exp(scores - top), 0.0)
    total = jnp.sum(weights, axis=1, keepdims=True)
    dprob = nt(cots, vals)
    mean = jnp.sum(weights * dprob, axis=1, keepdims=True) / jnp.where(total > 0.0, total, 1.0)
    spread = (weights * (dprob - mean)).astype(BF16)
    rounded = weights.astype(BF16)
    parts = (
        join_pair(nn(rounded, vals)),
        join_pair(nn(spread, keys)),
        join_pair(nn(rounded, keys)),
    )
    half = rows // 2
    for index, part in enumerate(parts):
        keep_ref[index] = part[:half]
        send_ref[index] = part[half:].astype(BF16)
    lane = lax.broadcasted_iota(jnp.int32, (rows, PAIR), 1)
    table = jnp.zeros((rows, PAIR), F32)
    for index, column in enumerate((top, total, mean)):
        table = jnp.where(lane == 2 * index, column[:rows], table)
        table = jnp.where(lane == 2 * index + 1, column[rows:], table)
    stat_ref[0] = table.T[:8]


def video_kernel(k_lo, k_hi, v_lo, v_hi, query_ref, grad_ref, out_ref, dq_ref, keep_ref, send_ref):
    queries, grads = query_ref[...], grad_ref[...]
    keys = block_diag(k_lo[...], k_hi[...])
    vals = block_diag(v_lo[...], v_hi[...])
    rows = keys.shape[0] // 2
    scores = nt(queries, keys) * SCALE
    probs = []
    for part in (scores[:, :rows], scores[:, rows:]):
        shifted = jnp.exp(part - jnp.max(part, axis=1, keepdims=True))
        probs.append(shifted / jnp.sum(shifted, axis=1, keepdims=True))
    rounded = jnp.concatenate([prob.astype(BF16) for prob in probs], axis=1)
    attended = nn(rounded, vals)
    out_ref[...] = attended.astype(BF16)
    dprob = nt(grads, vals)
    product = grads.astype(F32) * attended
    low = first_head(product.shape)
    proj = (
        jnp.sum(jnp.where(low, product, 0.0), axis=1, keepdims=True),
        jnp.sum(jnp.where(low, 0.0, product), axis=1, keepdims=True),
    )
    steps = jnp.concatenate(
        [
            (SCALE * probs[h] * (dprob[:, h * rows : (h + 1) * rows] - proj[h])).astype(BF16)
            for h in range(2)
        ],
        axis=1,
    )
    dq_ref[...] = nn(steps, keys).astype(BF16)
    half = rows // 2
    for index, part in enumerate((join_pair(tn(steps, queries)), join_pair(tn(rounded, grads)))):
        keep_ref[index] = part[:half]
        send_ref[index] = part[half:].astype(BF16)


def swap_lanes(x, shift):
    size = x.shape[-1]
    lane = lax.broadcasted_iota(jnp.int32, x.shape, x.ndim - 1)
    up = pltpu.roll(x, size - shift, x.ndim - 1)
    down = pltpu.roll(x, shift, x.ndim - 1)
    return jnp.where((lane & shift) == 0, up, down)


def merge_stats(mine, other, shift):
    other = swap_lanes(other, shift)
    top1, total1, mean1 = mine[0:2], mine[2:4], mine[4:6]
    top2, total2, mean2 = other[0:2], other[2:4], other[4:6]
    top = jnp.maximum(top1, top2)
    scale1, scale2 = jnp.exp(top1 - top), jnp.exp(top2 - top)
    part1, part2 = scale1 * total1, scale2 * total2
    total = part1 + part2
    mean = (part1 * mean1 + part2 * mean2) / jnp.where(total > 0.0, total, 1.0)
    shift1, shift2 = scale1 * (mean1 - mean), scale2 * (mean2 - mean)
    return top, total, mean, scale1, scale2, shift1, shift2


def merge_kernel(n_in, last, shift, *refs):
    mine_ref, other_ref = refs[:2]
    keeps, recvs = refs[2 : 2 + n_in], refs[2 + n_in : 2 + 2 * n_in]
    outs = refs[2 + 2 * n_in :]
    pairs, _, lanes = mine_ref.shape
    rows = keeps[0].shape[1]
    tables = []
    for pair in range(pairs):
        top, total, mean, scale1, scale2, shift1, shift2 = merge_stats(
            mine_ref[pair], other_ref[pair], shift
        )
        if last:
            inverse = 1.0 / total
            tables += [scale1 * inverse, scale2 * inverse, shift1 * inverse, shift2 * inverse]
        else:
            tables += [scale1, scale2, shift1, shift2]
            pad = jnp.zeros_like(top)
            outs[2][pair] = jnp.concatenate([top, total, mean, pad], axis=0)
    table = jnp.concatenate(tables, axis=0)
    if table.shape[0] < 128:
        table = jnp.concatenate([table, jnp.zeros((128 - table.shape[0], lanes), F32)], axis=0)
    table = table.T
    low = first_head((rows, PAIR))

    def fetch(group, index, cols):
        for ref in group:
            if index < ref.shape[0]:
                return ref[index, :, cols].astype(F32)
            index -= ref.shape[0]

    for pair in range(pairs):
        cols = slice(pair * PAIR, (pair + 1) * PAIR)

        def column(index):
            at = pair * 8 + 2 * index
            return jnp.where(low, table[:rows, at : at + 1], table[:rows, at + 1 : at + 2])

        scale1, scale2, shift1, shift2 = (column(index) for index in range(4))
        num1, step1, sum1, key1, val1 = (fetch(keeps, index, cols) for index in range(5))
        num2, step2, sum2, key2, val2 = (fetch(recvs, index, cols) for index in range(5))
        num = scale1 * num1 + scale2 * num2
        step = scale1 * step1 + shift1 * sum1 + scale2 * step2 + shift2 * sum2
        key, val = key1 + key2, val1 + val2
        if last:
            outs[0][:, cols] = num.astype(BF16)
            outs[1][:, cols] = (SCALE * step).astype(BF16)
            outs[2][:, cols] = key.astype(BF16)
            outs[3][:, cols] = val.astype(BF16)
        else:
            total = scale1 * sum1 + scale2 * sum2
            half = rows // 2
            for index, part in enumerate((num, step, total, key, val)):
                outs[0][index, :, cols] = part[:half]
                outs[1][index, :, cols] = part[half:].astype(BF16)


def final_kernel(shift, live_ref, q_lo, q_hi, c_lo, c_hi, key_ref, val_ref, mine_ref, other_ref, dk_ref, dv_ref):
    keys, vals = key_ref[...], val_ref[...]
    queries = block_diag(q_lo[...], q_hi[...])
    cots = block_diag(c_lo[...], c_hi[...])
    top, total, mean = merge_stats(mine_ref[0], other_ref[0], shift)[:3]
    inverse = 1.0 / total
    top, inverse, mean = (
        jnp.concatenate([item[0:1], item[1:2]], axis=1) for item in (top, inverse, mean)
    )
    scores = nt(keys, queries) * SCALE
    live = lax.broadcasted_iota(jnp.int32, scores.shape, 0) < live_ref[0]
    probs = jnp.where(live, jnp.exp(scores - top), 0.0) * inverse
    dprob = nt(vals, cots)
    steps = (SCALE * probs * (dprob - mean)).astype(BF16)
    dk_ref[...] = nn(steps, queries).astype(BF16)
    dv_ref[...] = nn(probs.astype(BF16), cots).astype(BF16)


def body(video_q, video_k, video_v, audio_q, audio_k, audio_v, video_length, video_cot, audio_cot):
    vid_rows, width = video_q.shape
    aud_rows = audio_q.shape[0]
    ctx_size, head_size = lax.axis_size("ctx"), lax.axis_size("head")
    ctx_index, head_index = lax.axis_index("ctx"), lax.axis_index("head")
    rows = aud_rows * ctx_size
    half = rows // 2
    pairs = width // PAIR
    bits = []
    while (1 << len(bits)) < ctx_size:
        bits.append(1 << len(bits))
    live = jnp.clip(video_length - ctx_index * vid_rows, 0, vid_rows).astype(jnp.int32)

    def flip(x, bit):
        return lax.ppermute(x, "ctx", [(i, i ^ bit) for i in range(ctx_size)])

    cot = video_cot[0]
    tok_rows = cot.shape[0]
    if head_size == 2:
        sent = lax.dynamic_slice_in_dim(cot, (1 - head_index) * width, width, 1)
        kept = lax.dynamic_slice_in_dim(cot, head_index * width, width, 1)
        got = lax.ppermute(sent, "head", [(0, 1), (1, 0)])
        video_grad = jnp.concatenate(
            [jnp.where(head_index == 0, kept, got), jnp.where(head_index == 0, got, kept)], axis=0
        )
    else:
        video_grad = lax.all_to_all(cot, "head", split_axis=1, concat_axis=0, tiled=True)

    gathered = jnp.concatenate([audio_q, audio_k, audio_v, audio_cot], axis=1)
    for bit in reversed(bits[1:]):
        gathered = jnp.concatenate([gathered, flip(gathered, bit)], axis=0)
    halves = (gathered, flip(gathered, bits[0]))

    def audio_spec(which):
        return pl.BlockSpec((half, PAIR), lambda pair: (0, which * pairs + pair))

    vid_spec = pl.BlockSpec((vid_rows, PAIR), lambda pair: (0, pair))
    scalar_spec = pl.BlockSpec(memory_space=pltpu.SMEM)
    stat_spec = pl.BlockSpec((1, 8, rows), lambda pair: (pair, 0, 0))
    stat_shape = jax.ShapeDtypeStruct((pairs, 8, rows), F32)

    def part_spec(count):
        return pl.BlockSpec((count, half, PAIR), lambda pair: (0, 0, pair))

    def part_shapes(count, part_rows):
        return [
            jax.ShapeDtypeStruct((count, part_rows, width), F32),
            jax.ShapeDtypeStruct((count, part_rows, width), BF16),
        ]

    product = 2 * vid_rows * 2 * rows * PAIR * pairs
    vid_bytes = 2 * vid_rows * width
    vid_shape = jax.ShapeDtypeStruct((vid_rows, width), BF16)

    def cost(matmuls, moved):
        return pl.CostEstimate(
            flops=matmuls * product, bytes_accessed=moved * vid_bytes, transcendentals=vid_rows * 2 * rows * pairs
        )

    stats, keep_a, send_a = pl.pallas_call(
        audio_kernel,
        grid=(pairs,),
        in_specs=[scalar_spec, audio_spec(0), audio_spec(0), audio_spec(3), audio_spec(3), vid_spec, vid_spec],
        out_specs=[stat_spec, part_spec(3), part_spec(3)],
        out_shape=[stat_shape, *part_shapes(3, half)],
        cost_estimate=cost(5, 5),
        name="audio_side",
    )(live, *halves, *halves, video_k, video_v)

    video_attended, grad_video_q, keep_b, send_b = pl.pallas_call(
        video_kernel,
        grid=(pairs,),
        in_specs=[audio_spec(1), audio_spec(1), audio_spec(2), audio_spec(2), vid_spec, vid_spec],
        out_specs=[vid_spec, vid_spec, part_spec(2), part_spec(2)],
        out_shape=[vid_shape, vid_shape, *part_shapes(2, half)],
        cost_estimate=cost(6, 6),
        name="video_side",
    )(*halves, *halves, video_q, video_grad)

    if head_size == 2:
        mine = lax.dynamic_slice_in_dim(video_attended, head_index * tok_rows, tok_rows, 0)
        theirs = lax.dynamic_slice_in_dim(video_attended, (1 - head_index) * tok_rows, tok_rows, 0)
        other = lax.ppermute(theirs, "head", [(0, 1), (1, 0)])
        video_out = jnp.concatenate(
            [jnp.where(head_index == 0, mine, other), jnp.where(head_index == 0, other, mine)], axis=1
        )[None]
    else:
        video_out = lax.all_to_all(video_attended, "head", split_axis=0, concat_axis=1, tiled=True)[None]

    keeps, sends = (keep_a, keep_b), (send_a, send_b)
    part_rows = half
    for bit in bits:
        last = bit == bits[-1]
        other_stats = flip(stats, bit)
        recvs = tuple(flip(send, bit) for send in sends)
        if last:
            out_shape = [jax.ShapeDtypeStruct((part_rows, width), BF16)] * 4
        else:
            out_shape = [*part_shapes(5, part_rows // 2), stat_shape]
        merged = pl.pallas_call(
            functools.partial(merge_kernel, len(keeps), last, part_rows),
            out_shape=out_shape,
            name=f"merge_{bit}",
        )(stats, other_stats, *keeps, *recvs)
        if last:
            audio_out, grad_audio_q, grad_audio_k, grad_audio_v = merged
        else:
            keep, send, stats = merged
            keeps, sends = (keep,), (send,)
            part_rows //= 2

    grad_video_k, grad_video_v = pl.pallas_call(
        functools.partial(final_kernel, part_rows),
        grid=(pairs,),
        in_specs=[
            scalar_spec,
            audio_spec(0),
            audio_spec(0),
            audio_spec(3),
            audio_spec(3),
            vid_spec,
            vid_spec,
            stat_spec,
            stat_spec,
        ],
        out_specs=[vid_spec, vid_spec],
        out_shape=[vid_shape, vid_shape],
        cost_estimate=cost(4, 4),
        name="audio_grads",
    )(live, *halves, *halves, video_k, video_v, stats, other_stats)
    return (
        video_out,
        audio_out,
        grad_video_q,
        grad_video_k,
        grad_video_v,
        grad_audio_q,
        grad_audio_k,
        grad_audio_v,
    )


def solution(mesh):
    wide = P("ctx", "head")
    tall = P("ctx", "head", None)
    return jax.shard_map(
        body,
        mesh=mesh,
        in_specs=(wide, wide, wide, wide, wide, wide, P(), tall, wide),
        out_specs=(tall, wide, wide, wide, wide, wide, wide, wide),
        check_vma=False,
    )
```

time: 373 us -> 98.5 us (0.26)
  blocking collectives: 143 us -> 0 us
  matrix products: 101 us -> 0 us
  Pallas kernels: 0 us -> 33.6 us
  other arithmetic: 26.2 us -> 1.95 us
  local copies, waits for them, and re-layouts: 29.6 us -> 6.47 us
  between operations: 18.3 us -> 1.45 us
  waiting for transfers between devices: 45.8 us -> 34.6 us
  starting transfers between devices: 8.28 us -> 18.8 us
    dot_general x147 -> x0, matrix products: 101 us -> none  [the longest x16 22.1 us: body(): jnp.einsum('vd,ad->va', head_slice(video_q, head_num), head_slice(audio_k...]
    all_gather x4 -> x0, blocking collectives: 81.8 us -> none  [the longest x1 24.2 us: body(): audio_queries = lax.all_gather(audio_q, 'ctx', axis=0, tiled=True)]
    reduce_scatter x1 -> x0, waiting for transfers between devices: 45.7 us -> none  [body(): lax.psum_scatter(jnp.concatenate([jnp.concatenate([key_grad, value_grad],...]
    ppermute x0 -> x15, waiting for transfers between devices: none -> 34.6 us  [the longest x13 28.3 us: flip(): return lax.ppermute(x, 'ctx', [(i, i ^ bit) for i in range(ctx_size)])]
    pallas_call x0 -> x7, Pallas kernels: none -> 33.6 us  [the longest x4 10.3 us: body(): pl.pallas_call(functools.partial(merge_kernel, len(keeps), last, part_row...]
    psum x1 -> x0, blocking collectives: 30.5 us -> none  [body(): numer_all, totals_all = lax.psum((numerators, totals), 'ctx')]
    pmax x1 -> x0, blocking collectives: 30.3 us -> none  [body(): global_max = lax.pmax(jnp.stack(local_max, axis=1), 'ctx')]
    reduce_sum x20 -> x0, other arithmetic: 22.6 us -> none  [the longest x16 15.3 us: body(): probs = shifted / jnp.sum(shifted, axis=1, keepdims=True)]
  transfers between devices with their start and end apart: 4 -> 15, of which waited for: 1 -> 9; matrix products, arithmetic and copies ran while one was open for 35% -> 2% of each run, Pallas kernels for 0% -> 19%
where the time goes in v1:
time: 98.5 us; the launch traced here: 96.9 us
  waiting for transfers between devices  34.6 us (35%)
  Pallas kernels  33.6 us (34%)
  starting transfers between devices  18.8 us (19%)
  local copies, waits for them, and re-layouts  6.47 us (7%)
  other arithmetic  1.95 us (2%)
  between operations  1.45 us (1%)
    ppermute x13, waiting for transfers between devices, flip(): return lax.ppermute(x, 'ctx', [(i, i ^ bit) for i in range(ctx_size)])  28.3 us
    ppermute x13, starting transfers between devices, flip(): return lax.ppermute(x, 'ctx', [(i, i ^ bit) for i in range(ctx_size)])  15.4 us
    pallas_call x4, Pallas kernels, body(): pl.pallas_call(functools.partial(merge_kernel, len(keeps), last, part_row...  10.3 us
    pallas_call x1, Pallas kernels, body(): pl.pallas_call(video_kernel, grid=(pairs,), in_specs=[audio_spec(1), audi...  9 us
    pallas_call x1, Pallas kernels, body(): pl.pallas_call(audio_kernel, grid=(pairs,), in_specs=[scalar_spec, audio_...  7.43 us
    pallas_call x1, Pallas kernels, body(): pl.pallas_call(functools.partial(final_kernel, part_rows), grid=(pairs,),...  6.86 us
    unnamed x39, local copies, waits for them, and re-layouts  6.43 us
    ppermute x1, waiting for transfers between devices, body(): got = lax.ppermute(sent, 'head', [(0, 1), (1, 0)])  6.3 us
  transfers between devices with their start and end apart: 15, of which 9 were waited for; matrix products, arithmetic and copies ran while one was open for 2% of the time, Pallas kernels for 19%

profile of v1, /device:TPU:0, one launch (start us, length us, event | category | flops | bytes accessed | tf_op | source)
XLA Modules:
  0.0 96.9 jit_solution(3759027473441549467)
XLA Ops:
  0.6 0.7 constant_dynamic-update-slice_fusion.3
  1.4 0.7 copy-done.16
  2.1 0.7 copy-done.17
  2.8 4.1 %collective-permute-start = (bf16[8,4096]{1,0:T(8,128)(2,1)S(1)}, bf16[8,4096]{1,0:T(8,128)(2,1)S(1)}, u32[]{:S(2)}, u32[]{:S(2)}) collective-permute-start(bf16[8,4096]{1,0:T(8,128)(2,1)S(1)} %constant_dynamic-update-slice_fusion), channel_id=1, source_target_pairs={{0,8},{1,9},{2,10},{3,11},{4,12},{5,13},{6,14},{7,15},{8,0},{9,1},... | collective-permute-start | bytes 196616 | tf_op jit(solution)/shard_map/ppermute | solution.py:220
  6.9 3.6 %collective-permute-done = bf16[8,4096]{1,0:T(8,128)(2,1)S(1)} collective-permute-done((bf16[8,4096]{1,0:T(8,128)(2,1)S(1)}, bf16[8,4096]{1,0:T(8,128)(2,1)S(1)}, u32[]{:S(2)}, u32[]{:S(2)}) %collective-permute-start) | collective-permute-done | bytes 65568 | tf_op jit(solution)/shard_map/ppermute | solution.py:220
  10.5 0.6 collective-permute-start.1
  11.2 4.4 %collective-permute-done.1 = bf16[16,4096]{1,0:T(8,128)(2,1)S(1)} collective-permute-done((bf16[16,4096]{1,0:T(8,128)(2,1)S(1)}, bf16[16,4096]{1,0:T(8,128)(2,1)S(1)}, u32[]{:S(2)}, u32[]{:S(2)}) %collective-permute-start.1) | collective-permute-done | bytes 131104 | tf_op jit(solution)/shard_map/ppermute | solution.py:220
  15.6 1.8 %collective-permute-start.2 = (bf16[32,4096]{1,0:T(8,128)(2,1)S(1)}, bf16[32,4096]{1,0:T(8,128)(2,1)S(1)}, u32[]{:S(2)}, u32[]{:S(2)}) collective-permute-start(bf16[32,4096]{1,0:T(8,128)(2,1)S(1)} %pad_maximum_fusion.2), channel_id=1, source_target_pairs={{0,2},{1,3},{2,0},{3,1},{4,6},{5,7},{6,4},{7,5},{8,10},{9,11},{10,... | collective-permute-start | bytes 786440 | tf_op jit(solution)/shard_map/ppermute | solution.py:220
  17.4 4.7 %collective-permute-done.2 = bf16[32,4096]{1,0:T(8,128)(2,1)S(1)} collective-permute-done((bf16[32,4096]{1,0:T(8,128)(2,1)S(1)}, bf16[32,4096]{1,0:T(8,128)(2,1)S(1)}, u32[]{:S(2)}, u32[]{:S(2)}) %collective-permute-start.2) | collective-permute-done | bytes 262176 | tf_op jit(solution)/shard_map/ppermute | solution.py:220
  22.1 0.1 collective-permute-start.3
  22.2 1.8 %collective-permute-start.4 = (bf16[128,1024]{1,0:T(8,128)(2,1)S(1)}, bf16[128,1024]{1,0:T(8,128)(2,1)S(1)}, u32[]{:S(2)}, u32[]{:S(2)}) collective-permute-start(bf16[128,1024]{1,0:T(8,128)(2,1)S(1)} %dynamic-slice_bitcast_fusion), channel_id=1, source_target_pairs={{0,16},{16,0},{1,17},{17,1},{2,18},{18,2},{3,19},{19,3},{4,20},{20... | collective-permute-start | bytes 786440 | tf_op jit(solution)/shard_map/ppermute | solution.py:227
  24.7 6.3 %collective-permute-done.4 = bf16[128,1024]{1,0:T(8,128)(2,1)S(1)} collective-permute-done((bf16[128,1024]{1,0:T(8,128)(2,1)S(1)}, bf16[128,1024]{1,0:T(8,128)(2,1)S(1)}, u32[]{:S(2)}, u32[]{:S(2)}) %collective-permute-start.4) | collective-permute-done | bytes 262176 | tf_op jit(solution)/shard_map/ppermute | solution.py:227
  31.0 0.1 bitcast_select_fusion.1
  31.1 0.8 copy-done.1
  31.9 7.4 %audio_side.1 = (f32[8,8,128]{2,1,0:T(8,128)}, f32[3,64,1024]{2,1,0:T(8,128)}, bf16[3,64,1024]{2,1,0:T(8,128)(2,1)}) custom-call(s32[1]{0:T(128)S(6)} %min.6.live_ref, bf16[64,4096]{1,0:T(8,128)(2,1)} %copy-done, bf16[64,4096]{1,0:T(8,128)(2,1)} %copy-done.1, bf16[64,4096]{1,0:T(8,128)(2,1)} %copy-done, bf16[64,4096]{1,0:T(8,128)(2,1)} %copy-done.1, ...), custom_call_target="tpu_custom_call" | custom-call | flops 671088640 | bytes 2621440 | tf_op jit(solution)/shard_map/audio_side/pallas_call | solution.py:265
  39.3 0.0 collective-permute-start.7
  39.3 0.8 pad_maximum_fusion.1.grad_ref
  40.2 9.0 %video_side.1 = (bf16[256,1024]{1,0:T(8,128)(2,1)}, bf16[256,1024]{1,0:T(8,128)(2,1)}, f32[2,64,1024]{2,1,0:T(8,128)}, bf16[2,64,1024]{2,1,0:T(8,128)(2,1)}) custom-call(bf16[64,4096]{1,0:T(8,128)(2,1)} %copy-done, bf16[64,4096]{1,0:T(8,128)(2,1)} %copy-done.1, bf16[64,4096]{1,0:T(8,128)(2,1)} %copy-done, bf16[64,4096]{1,0:T(8,128)(2,1)} %copy-done.1, ...), custom_call_target="tpu_custom_call" | custom-call | flops 805306368 | bytes 3145728 | tf_op jit(solution)/shard_map/video_side/pallas_call | solution.py:275
  49.2 0.6 collective-permute-start.8
  49.7 0.1 collective-permute-start.6
  49.8 1.3 %collective-permute-done.6.refs_1_ = f32[8,8,128]{2,1,0:T(8,128)S(1)} collective-permute-done((f32[8,8,128]{2,1,0:T(8,128)S(1)}, f32[8,8,128]{2,1,0:T(8,128)S(1)}, u32[]{:S(2)}, u32[]{:S(2)}) %collective-permute-start.6) | collective-permute-done | bytes 32800 | tf_op jit(solution)/shard_map/ppermute | solution.py:220
  51.2 0.0 copy-start.4
  51.2 0.6 copy-done.11
  51.7 0.1 copy-done.6
  51.8 0.1 copy-done.4
  52.0 3.5 %merge_1.1 = (f32[5,32,1024]{2,1,0:T(8,128)}, bf16[5,32,1024]{2,1,0:T(8,128)(2,1)}, f32[8,8,128]{2,1,0:T(8,128)}) custom-call(f32[8,8,128]{2,1,0:T(8,128)} %get-tuple-element.31.refs_0_, f32[8,8,128]{2,1,0:T(8,128)} %copy-done.11, f32[3,64,1024]{2,1,0:T(8,128)} %get-tuple-element.32.refs_2_, f32[2,64,1024]{2,1,0:T(8,128)} %get-tuple-element.33.refs_3_, ...), custom_call_target="tpu_custom_call" | custom-call | tf_op jit(solution)/shard_map/merge_1/pallas_call | solution.py:305
  55.4 1.7 %collective-permute-start.10 = (bf16[5,32,1024]{2,1,0:T(8,128)(2,1)}, bf16[5,32,1024]{2,1,0:T(8,128)(2,1)S(1)}, u32[]{:S(2)}, u32[]{:S(2)}) collective-permute-start(bf16[5,32,1024]{2,1,0:T(8,128)(2,1)} %get-tuple-element.38), channel_id=1, source_target_pairs={{0,2},{1,3},{2,0},{3,1},{4,6},{5,7},{6,4},{7,5},{8,10},{9,11},{10,... | collective-permute-start | bytes 983048 | tf_op jit(solution)/shard_map/ppermute | solution.py:220
  57.2 1.6 %collective-permute-start.5 = (bf16[128,1024]{1,0:T(8,128)(2,1)S(1)}, bf16[128,1024]{1,0:T(8,128)(2,1)S(1)}, u32[]{:S(2)}, u32[]{:S(2)}) collective-permute-start(bf16[128,1024]{1,0:T(8,128)(2,1)S(1)} %constant_dynamic-slice_fusion), channel_id=1, source_target_pairs={{0,16},{16,0},{1,17},{17,1},{2,18},{18,2},{3,19},{19,3},{4,20},{20... | collective-permute-start | bytes 786440 | tf_op jit(solution)/shard_map/ppermute | solution.py:288
  58.8 0.5 collective-permute-start.9
  59.3 7.1 %collective-permute-done.9.refs_1_ = f32[8,8,128]{2,1,0:T(8,128)S(1)} collective-permute-done((f32[8,8,128]{2,1,0:T(8,128)S(1)}, f32[8,8,128]{2,1,0:T(8,128)S(1)}, u32[]{:S(2)}, u32[]{:S(2)}) %collective-permute-start.9) | collective-permute-done | bytes 32800 | tf_op jit(solution)/shard_map/ppermute | solution.py:220
  66.3 0.6 copy-done.14
  67.0 0.1 copy-done.5
  67.1 2.6 %merge_2.1 = (f32[5,16,1024]{2,1,0:T(8,128)}, bf16[5,16,1024]{2,1,0:T(8,128)(2,1)}, f32[8,8,128]{2,1,0:T(8,128)}) custom-call(f32[8,8,128]{2,1,0:T(8,128)} %get-tuple-element.36.refs_0_, f32[8,8,128]{2,1,0:T(8,128)} %copy-done.14, f32[5,32,1024]{2,1,0:T(8,128)} %get-tuple-element.37.refs_2_, bf16[5,32,1024]{2,1,0:T(8,128)(2,1)} %copy-done.5), custom_call_target="tpu_custom_call" | custom-call | tf_op jit(solution)/shard_map/merge_2/pallas_call | solution.py:305
  69.7 0.8 collective-permute-start.11
  70.5 1.2 %collective-permute-start.12 = (bf16[5,16,1024]{2,1,0:T(8,128)(2,1)}, bf16[5,16,1024]{2,1,0:T(8,128)(2,1)S(1)}, u32[]{:S(2)}, u32[]{:S(2)}) collective-permute-start(bf16[5,16,1024]{2,1,0:T(8,128)(2,1)} %get-tuple-element.41), channel_id=1, source_target_pairs={{0,4},{1,5},{2,6},{3,7},{4,0},{5,1},{6,2},{7,3},{8,12},{9,13},{10,... | collective-permute-start | bytes 491528 | tf_op jit(solution)/shard_map/ppermute | solution.py:220
  71.8 0.1 broadcast_select_fusion.1
  71.9 2.3 %collective-permute-done.11.refs_1_ = f32[8,8,128]{2,1,0:T(8,128)S(1)} collective-permute-done((f32[8,8,128]{2,1,0:T(8,128)}, f32[8,8,128]{2,1,0:T(8,128)S(1)}, u32[]{:S(2)}, u32[]{:S(2)}) %collective-permute-start.11) | collective-permute-done | bytes 32800 | tf_op jit(solution)/shard_map/ppermute | solution.py:220
  74.2 2.2 %collective-permute-done.12.refs_3_ = bf16[5,16,1024]{2,1,0:T(8,128)(2,1)S(1)} collective-permute-done((bf16[5,16,1024]{2,1,0:T(8,128)(2,1)}, bf16[5,16,1024]{2,1,0:T(8,128)(2,1)S(1)}, u32[]{:S(2)}, u32[]{:S(2)}) %collective-permute-start.12) | collective-permute-done | bytes 163872 | tf_op jit(solution)/shard_map/ppermute | solution.py:220
  76.4 0.7 copy-done.7
  77.1 2.2 %merge_4.1 = (f32[5,8,1024]{2,1,0:T(8,128)}, bf16[5,8,1024]{2,1,0:T(8,128)(2,1)}, f32[8,8,128]{2,1,0:T(8,128)}) custom-call(f32[8,8,128]{2,1,0:T(8,128)} %get-tuple-element.39.refs_0_, f32[8,8,128]{2,1,0:T(8,128)} %copy-done.13, f32[5,16,1024]{2,1,0:T(8,128)} %get-tuple-element.40.refs_2_, bf16[5,16,1024]{2,1,0:T(8,128)(2,1)} %copy-done.7), custom_call_target="tpu_custom_call" | custom-call | tf_op jit(solution)/shard_map/merge_4/pallas_call | solution.py:305
  79.3 3.9 %collective-permute-start.13 = (f32[8,8,128]{2,1,0:T(8,128)}, f32[8,8,128]{2,1,0:T(8,128)S(1)}, u32[]{:S(2)}, u32[]{:S(2)}) collective-permute-start(f32[8,8,128]{2,1,0:T(8,128)} %get-tuple-element.42.refs_0_.mine_ref), channel_id=1, source_target_pairs={{0,8},{1,9},{2,10},{3,11},{4,12},{5,13},{6,14},{7,15},{8,0},{9,1},... | collective-permute-start | bytes 98312 | tf_op jit(solution)/shard_map/ppermute | solution.py:220
  83.3 0.0 collective-permute-start.14
  83.3 0.8 maximum_bitcast_fusion
  84.1 2.7 %collective-permute-done.13.refs_1_.other_ref = f32[8,8,128]{2,1,0:T(8,128)S(1)} collective-permute-done((f32[8,8,128]{2,1,0:T(8,128)}, f32[8,8,128]{2,1,0:T(8,128)S(1)}, u32[]{:S(2)}, u32[]{:S(2)}) %collective-permute-start.13) | collective-permute-done | bytes 32800 | tf_op jit(solution)/shard_map/ppermute | solution.py:220
  86.8 0.6 copy-done.8
  87.4 6.9 %audio_grads.1 = (bf16[256,1024]{1,0:T(8,128)(2,1)}, bf16[256,1024]{1,0:T(8,128)(2,1)}) custom-call(s32[1]{0:T(128)S(6)} %min.6.live_ref, bf16[64,4096]{1,0:T(8,128)(2,1)} %copy-done, bf16[64,4096]{1,0:T(8,128)(2,1)} %copy-done.1, bf16[64,4096]{1,0:T(8,128)(2,1)} %copy-done, bf16[64,4096]{1,0:T(8,128)(2,1)} %copy-done.1, bf16[256,1024]{1,0:T(8,128)(2,1)} %key_ref.3, ...), custom_call_target="tpu_custom_call" | custom-call | flops 536870912 | bytes 2097152 | tf_op jit(solution)/shard_map/audio_grads/pallas_call | solution.py:317
  94.3 0.6 copy-done.9
  94.9 2.0 %merge_8.1 = (bf16[8,1024]{1,0:T(8,128)(2,1)}, bf16[8,1024]{1,0:T(8,128)(2,1)}, bf16[8,1024]{1,0:T(8,128)(2,1)}, bf16[8,1024]{1,0:T(8,128)(2,1)}) custom-call(f32[8,8,128]{2,1,0:T(8,128)} %get-tuple-element.42.refs_0_.mine_ref, f32[8,8,128]{2,1,0:T(8,128)} %copy-done.8, f32[5,8,1024]{2,1,0:T(8,128)} %get-tuple-element.43.refs_2_, bf16[5,8,1024]{2,1,0:T(8,128)(2,1)} %copy-done.9), custom_call_target="tpu_custom_call" | custom-call | tf_op jit(solution)/shard_map/merge_8/pallas_call | solution.py:305
  (38 shorter events, 0.2 us)
Async XLA Ops:
  0.6 0.7 copy-start.15
  1.4 0.7 copy-start.16
  2.1 0.7 copy-start.17
  2.8 7.7 %collective-permute-start = (bf16[8,4096]{1,0:T(8,128)(2,1)S(1)}, bf16[8,4096]{1,0:T(8,128)(2,1)S(1)}, u32[]{:S(2)}, u32[]{:S(2)}) collective-permute-start(bf16[8,4096]{1,0:T(8,128)(2,1)S(1)} %constant_dynamic-update-slice_fusion), channel_id=1, source_target_pairs={{0,8},{1,9},{2,10},{3,11},{4,12},{5,13},{6,14},{7,15},{8,0},{9,1},... | collective-permute-start | bytes 196616 | tf_op jit(solution)/shard_map/ppermute | solution.py:220
  10.5 5.0 %collective-permute-start.1 = (bf16[16,4096]{1,0:T(8,128)(2,1)S(1)}, bf16[16,4096]{1,0:T(8,128)(2,1)S(1)}, u32[]{:S(2)}, u32[]{:S(2)}) collective-permute-start(bf16[16,4096]{1,0:T(8,128)(2,1)S(1)} %pad_maximum_fusion.3), channel_id=1, source_target_pairs={{0,4},{1,5},{2,6},{3,7},{4,0},{5,1},{6,2},{7,3},{8,12},{9,13},{10,... | collective-permute-start | bytes 393224 | tf_op jit(solution)/shard_map/ppermute | solution.py:220
  15.6 6.4 %collective-permute-start.2 = (bf16[32,4096]{1,0:T(8,128)(2,1)S(1)}, bf16[32,4096]{1,0:T(8,128)(2,1)S(1)}, u32[]{:S(2)}, u32[]{:S(2)}) collective-permute-start(bf16[32,4096]{1,0:T(8,128)(2,1)S(1)} %pad_maximum_fusion.2), channel_id=1, source_target_pairs={{0,2},{1,3},{2,0},{3,1},{4,6},{5,7},{6,4},{7,5},{8,10},{9,11},{10,... | collective-permute-start | bytes 786440 | tf_op jit(solution)/shard_map/ppermute | solution.py:220
  17.4 4.8 %copy-start.2 = (bf16[1,128,2048]{2,1,0:T(8,128)(2,1)S(1)}, bf16[1,128,2048]{2,1,0:T(8,128)(2,1)}, u32[]{:S(2)}) copy-start(bf16[1,128,2048]{2,1,0:T(8,128)(2,1)} %param.16) | copy-start | bytes 1572868
  22.1 9.0 %copy-start = (bf16[64,4096]{1,0:T(8,128)(2,1)}, bf16[64,4096]{1,0:T(8,128)(2,1)S(1)}, u32[]{:S(2)}) copy-start(bf16[64,4096]{1,0:T(8,128)(2,1)S(1)} %pad_maximum_fusion.k_lo.v_lo.q_lo.c_lo) | copy-start | bytes 1572868
  22.1 9.0 %collective-permute-start.3 = (bf16[64,4096]{1,0:T(8,128)(2,1)S(1)}, bf16[64,4096]{1,0:T(8,128)(2,1)S(1)}, u32[]{:S(2)}, u32[]{:S(2)}) collective-permute-start(bf16[64,4096]{1,0:T(8,128)(2,1)S(1)} %pad_maximum_fusion.k_lo.v_lo.q_lo.c_lo), channel_id=1, source_target_pairs={{0,1},{1,0},{2,3},{3,2},{4,5},{5,4},{6,7},{7,6},{8,9},{9,8},{10,11... | collective-permute-start | bytes 1572872 | tf_op jit(solution)/shard_map/ppermute | solution.py:220
  22.2 8.8 %collective-permute-start.4 = (bf16[128,1024]{1,0:T(8,128)(2,1)S(1)}, bf16[128,1024]{1,0:T(8,128)(2,1)S(1)}, u32[]{:S(2)}, u32[]{:S(2)}) collective-permute-start(bf16[128,1024]{1,0:T(8,128)(2,1)S(1)} %dynamic-slice_bitcast_fusion), channel_id=1, source_target_pairs={{0,16},{16,0},{1,17},{17,1},{2,18},{18,2},{3,19},{19,3},{4,20},{20... | collective-permute-start | bytes 786440 | tf_op jit(solution)/shard_map/ppermute | solution.py:227
  31.1 0.8 copy-start.1
  39.3 11.8 %collective-permute-start.7 = (bf16[3,64,1024]{2,1,0:T(8,128)(2,1)}, bf16[3,64,1024]{2,1,0:T(8,128)(2,1)S(1)}, u32[]{:S(2)}, u32[]{:S(2)}) collective-permute-start(bf16[3,64,1024]{2,1,0:T(8,128)(2,1)} %get-tuple-element.34), channel_id=1, source_target_pairs={{0,1},{1,0},{2,3},{3,2},{4,5},{5,4},{6,7},{7,6},{8,9},{9,8},{10,11... | collective-permute-start | bytes 1179656 | tf_op jit(solution)/shard_map/ppermute | solution.py:220
  40.2 9.6 %copy-start.10 = (f32[8,8,128]{2,1,0:T(8,128)S(1)}, f32[8,8,128]{2,1,0:T(8,128)}, u32[]{:S(2)}) copy-start(f32[8,8,128]{2,1,0:T(8,128)} %get-tuple-element.31.refs_0_) | copy-start | bytes 98308
  49.2 2.0 %collective-permute-start.8 = (bf16[2,64,1024]{2,1,0:T(8,128)(2,1)}, bf16[2,64,1024]{2,1,0:T(8,128)(2,1)S(1)}, u32[]{:S(2)}, u32[]{:S(2)}) collective-permute-start(bf16[2,64,1024]{2,1,0:T(8,128)(2,1)} %get-tuple-element.35), channel_id=1, source_target_pairs={{0,1},{1,0},{2,3},{3,2},{4,5},{5,4},{6,7},{7,6},{8,9},{9,8},{10,11... | collective-permute-start | bytes 786440 | tf_op jit(solution)/shard_map/ppermute | solution.py:220
  49.7 1.4 %collective-permute-start.6 = (f32[8,8,128]{2,1,0:T(8,128)S(1)}, f32[8,8,128]{2,1,0:T(8,128)S(1)}, u32[]{:S(2)}, u32[]{:S(2)}) collective-permute-start(f32[8,8,128]{2,1,0:T(8,128)S(1)} %copy-done.10), channel_id=1, source_target_pairs={{0,1},{1,0},{2,3},{3,2},{4,5},{5,4},{6,7},{7,6},{8,9},{9,8},{10,11... | collective-permute-start | bytes 98312 | tf_op jit(solution)/shard_map/ppermute | solution.py:220
  51.1 0.6 copy-start.11
  51.1 0.7 copy-start.6
  51.2 0.8 copy-start.4
  52.0 5.2 %copy-start.3 = (bf16[256,1024]{1,0:T(8,128)(2,1)S(1)}, bf16[256,1024]{1,0:T(8,128)(2,1)}, u32[]{:S(2)}) copy-start(bf16[256,1024]{1,0:T(8,128)(2,1)} %get-tuple-element.30) | copy-start | bytes 1572868
  55.4 10.9 %collective-permute-start.10 = (bf16[5,32,1024]{2,1,0:T(8,128)(2,1)}, bf16[5,32,1024]{2,1,0:T(8,128)(2,1)S(1)}, u32[]{:S(2)}, u32[]{:S(2)}) collective-permute-start(bf16[5,32,1024]{2,1,0:T(8,128)(2,1)} %get-tuple-element.38), channel_id=1, source_target_pairs={{0,2},{1,3},{2,0},{3,1},{4,6},{5,7},{6,4},{7,5},{8,10},{9,11},{10,... | collective-permute-start | bytes 983048 | tf_op jit(solution)/shard_map/ppermute | solution.py:220
  57.1 1.6 %copy-start.12 = (f32[8,8,128]{2,1,0:T(8,128)S(1)}, f32[8,8,128]{2,1,0:T(8,128)}, u32[]{:S(2)}) copy-start(f32[8,8,128]{2,1,0:T(8,128)} %get-tuple-element.36.refs_0_) | copy-start | bytes 98308
  57.2 14.6 %collective-permute-start.5 = (bf16[128,1024]{1,0:T(8,128)(2,1)S(1)}, bf16[128,1024]{1,0:T(8,128)(2,1)S(1)}, u32[]{:S(2)}, u32[]{:S(2)}) collective-permute-start(bf16[128,1024]{1,0:T(8,128)(2,1)S(1)} %constant_dynamic-slice_fusion), channel_id=1, source_target_pairs={{0,16},{16,0},{1,17},{17,1},{2,18},{18,2},{3,19},{19,3},{4,20},{20... | collective-permute-start | bytes 786440 | tf_op jit(solution)/shard_map/ppermute | solution.py:288
  58.8 7.6 %collective-permute-start.9 = (f32[8,8,128]{2,1,0:T(8,128)S(1)}, f32[8,8,128]{2,1,0:T(8,128)S(1)}, u32[]{:S(2)}, u32[]{:S(2)}) collective-permute-start(f32[8,8,128]{2,1,0:T(8,128)S(1)} %copy-done.12), channel_id=1, source_target_pairs={{0,2},{1,3},{2,0},{3,1},{4,6},{5,7},{6,4},{7,5},{8,10},{9,11},{10,... | collective-permute-start | bytes 98312 | tf_op jit(solution)/shard_map/ppermute | solution.py:220
  66.3 0.6 copy-start.14
  66.3 0.7 copy-start.5
  69.7 4.5 %collective-permute-start.11 = (f32[8,8,128]{2,1,0:T(8,128)}, f32[8,8,128]{2,1,0:T(8,128)S(1)}, u32[]{:S(2)}, u32[]{:S(2)}) collective-permute-start(f32[8,8,128]{2,1,0:T(8,128)} %get-tuple-element.39.refs_0_), channel_id=1, source_target_pairs={{0,4},{1,5},{2,6},{3,7},{4,0},{5,1},{6,2},{7,3},{8,12},{9,13},{10,... | collective-permute-start | bytes 98312 | tf_op jit(solution)/shard_map/ppermute | solution.py:220
  70.5 5.9 %collective-permute-start.12 = (bf16[5,16,1024]{2,1,0:T(8,128)(2,1)}, bf16[5,16,1024]{2,1,0:T(8,128)(2,1)S(1)}, u32[]{:S(2)}, u32[]{:S(2)}) collective-permute-start(bf16[5,16,1024]{2,1,0:T(8,128)(2,1)} %get-tuple-element.41), channel_id=1, source_target_pairs={{0,4},{1,5},{2,6},{3,7},{4,0},{5,1},{6,2},{7,3},{8,12},{9,13},{10,... | collective-permute-start | bytes 491528 | tf_op jit(solution)/shard_map/ppermute | solution.py:220
  74.2 2.2 %copy-start.13 = (f32[8,8,128]{2,1,0:T(8,128)}, f32[8,8,128]{2,1,0:T(8,128)S(1)}, u32[]{:S(2)}) copy-start(f32[8,8,128]{2,1,0:T(8,128)S(1)} %collective-permute-done.11.refs_1_) | copy-start | bytes 98308
  76.4 0.7 copy-start.7
  79.3 7.4 %collective-permute-start.13 = (f32[8,8,128]{2,1,0:T(8,128)}, f32[8,8,128]{2,1,0:T(8,128)S(1)}, u32[]{:S(2)}, u32[]{:S(2)}) collective-permute-start(f32[8,8,128]{2,1,0:T(8,128)} %get-tuple-element.42.refs_0_.mine_ref), channel_id=1, source_target_pairs={{0,8},{1,9},{2,10},{3,11},{4,12},{5,13},{6,14},{7,15},{8,0},{9,1},... | collective-permute-start | bytes 98312 | tf_op jit(solution)/shard_map/ppermute | solution.py:220
  83.3 11.0 %collective-permute-start.14 = (bf16[5,8,1024]{2,1,0:T(8,128)(2,1)}, bf16[5,8,1024]{2,1,0:T(8,128)(2,1)S(1)}, u32[]{:S(2)}, u32[]{:S(2)}) collective-permute-start(bf16[5,8,1024]{2,1,0:T(8,128)(2,1)} %get-tuple-element.44), channel_id=1, source_target_pairs={{0,8},{1,9},{2,10},{3,11},{4,12},{5,13},{6,14},{7,15},{8,0},{9,1},... | collective-permute-start | bytes 245768 | tf_op jit(solution)/shard_map/ppermute | solution.py:220
  86.8 0.6 copy-start.8
  94.3 0.6 copy-start.9

commit v2 on v1

v2 whole, which is shorter than its diff:
```python
import functools

import jax
import jax.numpy as jnp
from jax import lax
from jax.experimental import pallas as pl
from jax.experimental.pallas import tpu as pltpu
from jax.sharding import PartitionSpec as P


HEAD_DIM = 64
PAIR = 2 * HEAD_DIM
SCALE = HEAD_DIM ** (-0.5)
NEG = -1e30
GROUP = 2
PARAMS = pltpu.CompilerParams(vmem_limit_bytes=12 * 1024 * 1024)
F32 = jnp.float32
BF16 = jnp.bfloat16


def nt(x, y):
    return lax.dot_general(x, y, (((1,), (1,)), ((), ())), preferred_element_type=F32)


def nn(x, y):
    return jnp.dot(x, y, preferred_element_type=F32)


def tn(x, y):
    return lax.dot_general(x, y, (((0,), (0,)), ((), ())), preferred_element_type=F32)


def first_head(shape):
    return lax.broadcasted_iota(jnp.int32, shape, len(shape) - 1) < HEAD_DIM


def block_diag(low, high):
    rows = jnp.concatenate([low, high], axis=0)
    keep = first_head(rows.shape)
    zero = jnp.zeros_like(rows)
    return jnp.concatenate([jnp.where(keep, rows, zero), jnp.where(keep, zero, rows)], axis=0)


def join_pair(stacked):
    rows = stacked.shape[0] // 2
    return jnp.where(first_head((rows, PAIR)), stacked[:rows], stacked[rows:])


def pair_cols(pair):
    return slice(pair * PAIR, (pair + 1) * PAIR)


def audio_kernel(live_ref, q_lo, q_hi, c_lo, c_hi, key_ref, val_ref, stat_ref, keep_ref, send_ref):
    for pair in range(stat_ref.shape[0]):
        cols = pair_cols(pair)
        keys, vals = key_ref[:, cols], val_ref[:, cols]
        queries = block_diag(q_lo[:, cols], q_hi[:, cols])
        cots = block_diag(c_lo[:, cols], c_hi[:, cols])
        rows = queries.shape[0] // 2
        scores = nt(queries, keys) * SCALE
        live = lax.broadcasted_iota(jnp.int32, scores.shape, 1) < live_ref[0]
        top = jnp.max(jnp.where(live, scores, NEG), axis=1, keepdims=True)
        weights = jnp.where(live, jnp.exp(scores - top), 0.0)
        total = jnp.sum(weights, axis=1, keepdims=True)
        dprob = nt(cots, vals)
        mean = jnp.sum(weights * dprob, axis=1, keepdims=True) / jnp.where(total > 0.0, total, 1.0)
        spread = (weights * (dprob - mean)).astype(BF16)
        rounded = weights.astype(BF16)
        parts = (
            join_pair(nn(rounded, vals)),
            join_pair(nn(spread, keys)),
            join_pair(nn(rounded, keys)),
        )
        half = rows // 2
        for index, part in enumerate(parts):
            keep_ref[index, :, cols] = part[:half]
            send_ref[index, :, cols] = part[half:].astype(BF16)
        lane = lax.broadcasted_iota(jnp.int32, (rows, PAIR), 1)
        table = jnp.zeros((rows, PAIR), F32)
        for index, column in enumerate((top, total, mean)):
            table = jnp.where(lane == 2 * index, column[:rows], table)
            table = jnp.where(lane == 2 * index + 1, column[rows:], table)
        stat_ref[pair] = table.T[:8]


def video_kernel(head_ref, k_lo, k_hi, v_lo, v_hi, query_ref, grad_ref, *outs):
    *out_refs, dq_ref, keep_ref, send_ref = outs
    for pair in range(query_ref.shape[1] // PAIR):
        cols = pair_cols(pair)
        queries, grads = query_ref[:, cols], grad_ref[:, cols]
        keys = block_diag(k_lo[:, cols], k_hi[:, cols])
        vals = block_diag(v_lo[:, cols], v_hi[:, cols])
        rows = keys.shape[0] // 2
        scores = nt(queries, keys) * SCALE
        probs = []
        for part in (scores[:, :rows], scores[:, rows:]):
            shifted = jnp.exp(part - jnp.max(part, axis=1, keepdims=True))
            probs.append(shifted * (1.0 / jnp.sum(shifted, axis=1, keepdims=True)))
        rounded = jnp.concatenate([prob.astype(BF16) for prob in probs], axis=1)
        attended = nn(rounded, vals)
        if len(out_refs) == 1:
            out_refs[0][:, cols] = attended.astype(BF16)
        else:
            tok_rows = attended.shape[0] // 2
            upper, lower = attended[:tok_rows].astype(BF16), attended[tok_rows:].astype(BF16)
            is_first = jnp.full(upper.shape, head_ref[0], jnp.int32) == 0
            out_refs[0][:, cols] = jnp.where(is_first, upper, lower)
            out_refs[1][:, cols] = jnp.where(is_first, lower, upper)
        dprob = nt(grads, vals)
        product = grads.astype(F32) * attended
        low = first_head(product.shape)
        proj = (
            jnp.sum(jnp.where(low, product, 0.0), axis=1, keepdims=True),
            jnp.sum(jnp.where(low, 0.0, product), axis=1, keepdims=True),
        )
        steps = jnp.concatenate(
            [
                (SCALE * probs[h] * (dprob[:, h * rows : (h + 1) * rows] - proj[h])).astype(BF16)
                for h in range(2)
            ],
            axis=1,
        )
        dq_ref[:, cols] = nn(steps, keys).astype(BF16)
        half = rows // 2
        for index, part in enumerate((join_pair(tn(steps, queries)), join_pair(tn(rounded, grads)))):
            keep_ref[index, :, cols] = part[:half]
            send_ref[index, :, cols] = part[half:].astype(BF16)


def swap_lanes(x, shift):
    size = x.shape[-1]
    lane = lax.broadcasted_iota(jnp.int32, x.shape, x.ndim - 1)
    up = pltpu.roll(x, size - shift, x.ndim - 1)
    down = pltpu.roll(x, shift, x.ndim - 1)
    return jnp.where((lane & shift) == 0, up, down)


def merge_stats(mine, other, shift):
    other = swap_lanes(other, shift)
    top1, total1, mean1 = mine[0:2], mine[2:4], mine[4:6]
    top2, total2, mean2 = other[0:2], other[2:4], other[4:6]
    top = jnp.maximum(top1, top2)
    scale1, scale2 = jnp.exp(top1 - top), jnp.exp(top2 - top)
    part1, part2 = scale1 * total1, scale2 * total2
    total = part1 + part2
    mean = (part1 * mean1 + part2 * mean2) / jnp.where(total > 0.0, total, 1.0)
    shift1, shift2 = scale1 * (mean1 - mean), scale2 * (mean2 - mean)
    return top, total, mean, scale1, scale2, shift1, shift2


def stats_kernel(shift, mine_ref, other_ref, out_ref):
    for pair in range(mine_ref.shape[0]):
        top, total, mean = merge_stats(mine_ref[pair], other_ref[pair], shift)[:3]
        out_ref[pair] = jnp.concatenate([top, total, mean, jnp.zeros_like(top)], axis=0)


def merge_tables(pairs, factors):
    tables = []
    for pair in range(pairs):
        tables += factors(pair)
    table = jnp.concatenate(tables, axis=0)
    if table.shape[0] < 128:
        pad = jnp.zeros((128 - table.shape[0], table.shape[1]), F32)
        table = jnp.concatenate([table, pad], axis=0)
    return table.T


def merged_parts(table, pair, keeps, recvs):
    cols = pair_cols(pair)
    rows = keeps[0].shape[1]
    low = first_head((rows, PAIR))

    def column(index):
        at = pair * 8 + 2 * index
        return jnp.where(low, table[:rows, at : at + 1], table[:rows, at + 1 : at + 2])

    def fetch(group, index):
        for ref in group:
            if index < ref.shape[0]:
                return ref[index, :, cols].astype(F32)
            index -= ref.shape[0]

    scale1, scale2, shift1, shift2 = (column(index) for index in range(4))
    num1, step1, sum1, key1, val1 = (fetch(keeps, index) for index in range(5))
    num2, step2, sum2, key2, val2 = (fetch(recvs, index) for index in range(5))
    num = scale1 * num1 + scale2 * num2
    step = scale1 * step1 + shift1 * sum1 + scale2 * step2 + shift2 * sum2
    return num, step, scale1 * sum1 + scale2 * sum2, key1 + key2, val1 + val2


def merge_kernel(n_in, shift, *refs):
    mine_ref, other_ref = refs[:2]
    keeps, recvs = refs[2 : 2 + n_in], refs[2 + n_in : 2 + 2 * n_in]
    keep_ref, send_ref = refs[2 + 2 * n_in :]
    pairs = mine_ref.shape[0]
    half = keeps[0].shape[1] // 2
    table = merge_tables(
        pairs, lambda pair: list(merge_stats(mine_ref[pair], other_ref[pair], shift)[3:])
    )
    for pair in range(pairs):
        cols = pair_cols(pair)
        for index, part in enumerate(merged_parts(table, pair, keeps, recvs)):
            keep_ref[index, :, cols] = part[:half]
            send_ref[index, :, cols] = part[half:].astype(BF16)


def settle_kernel(n_in, shift, *refs):
    mine_ref, other_ref, all_ref = refs[:3]
    keeps, recvs = refs[3 : 3 + n_in], refs[3 + n_in : 3 + 2 * n_in]
    outs = refs[3 + 2 * n_in :]
    pairs = mine_ref.shape[0]
    rows = outs[0].shape[1]

    def factors(pair):
        both = all_ref[pair]
        top, inverse, mean = both[0:2], 1.0 / both[2:4], both[4:6]
        mine, other = mine_ref[pair], swap_lanes(other_ref[pair], shift)
        scales = [jnp.exp(item[0:2] - top) * inverse for item in (mine, other)]
        return scales + [
            scale * (item[4:6] - mean) for scale, item in zip(scales, (mine, other))
        ]

    table = merge_tables(pairs, factors)
    for pair in range(pairs):
        cols = pair_cols(pair)
        num, step, _, key, val = merged_parts(table, pair, keeps, recvs)
        for index, part in enumerate((num, SCALE * step, key, val)):
            for slot, out in enumerate(outs):
                out[index, :, cols] = part[slot * rows : (slot + 1) * rows].astype(out.dtype)


def add_kernel(*refs):
    parts, outs = refs[:-4], refs[-4:]
    for index, out in enumerate(outs):
        total = parts[0][index].astype(F32)
        for part in parts[1:]:
            total = total + part[index].astype(F32)
        out[...] = total.astype(BF16)


def final_kernel(live_ref, q_lo, q_hi, c_lo, c_hi, key_ref, val_ref, stat_ref, dk_ref, dv_ref):
    for pair in range(stat_ref.shape[0]):
        cols = pair_cols(pair)
        keys, vals = key_ref[:, cols], val_ref[:, cols]
        queries = block_diag(q_lo[:, cols], q_hi[:, cols])
        cots = block_diag(c_lo[:, cols], c_hi[:, cols])
        stat = stat_ref[pair]
        top, inverse, mean = stat[0:2], 1.0 / stat[2:4], stat[4:6]
        top, inverse, mean = (
            jnp.concatenate([item[0:1], item[1:2]], axis=1) for item in (top, inverse, mean)
        )
        scores = nt(keys, queries) * SCALE
        live = lax.broadcasted_iota(jnp.int32, scores.shape, 0) < live_ref[0]
        probs = jnp.where(live, jnp.exp(scores - top), 0.0) * inverse
        dprob = nt(vals, cots)
        steps = (SCALE * probs * (dprob - mean)).astype(BF16)
        dk_ref[:, cols] = nn(steps, queries).astype(BF16)
        dv_ref[:, cols] = nn(probs.astype(BF16), cots).astype(BF16)


def pack_kernel(*refs):
    width = refs[0].shape[1]
    for index, ref in enumerate(refs[:-1]):
        refs[-1][:, index * width : (index + 1) * width] = ref[...]


def body(video_q, video_k, video_v, audio_q, audio_k, audio_v, video_length, video_cot, audio_cot):
    vid_rows, width = video_q.shape
    aud_rows = audio_q.shape[0]
    ctx_size, head_size = lax.axis_size("ctx"), lax.axis_size("head")
    ctx_index, head_index = lax.axis_index("ctx"), lax.axis_index("head")
    rows = aud_rows * ctx_size
    half = rows // 2
    pairs = width // PAIR
    group = min(GROUP, pairs)
    steps = pairs // group
    wide = group * PAIR
    bits = []
    while (1 << len(bits)) < ctx_size:
        bits.append(1 << len(bits))
    live = jnp.clip(video_length - ctx_index * vid_rows, 0, vid_rows).astype(jnp.int32)

    def flip(x, bit):
        return lax.ppermute(x, "ctx", [(i, i ^ bit) for i in range(ctx_size)])

    cot = video_cot[0]
    tok_rows = cot.shape[0]
    if head_size == 2:
        sent = lax.dynamic_slice_in_dim(cot, (1 - head_index) * width, width, 1)
        kept = lax.dynamic_slice_in_dim(cot, head_index * width, width, 1)
        got = lax.ppermute(sent, "head", [(0, 1), (1, 0)])
        video_grad = jnp.concatenate(
            [jnp.where(head_index == 0, kept, got), jnp.where(head_index == 0, got, kept)], axis=0
        )
    else:
        video_grad = lax.all_to_all(cot, "head", split_axis=1, concat_axis=0, tiled=True)

    gathered = pl.pallas_call(
        pack_kernel,
        out_shape=jax.ShapeDtypeStruct((aud_rows, 4 * width), BF16),
        compiler_params=PARAMS,
        name="pack",
    )(audio_q, audio_k, audio_v, audio_cot)
    quarters = [gathered]
    for bit in (bits[-1], bits[-2], bits[-1] | bits[-2]):
        quarters.append(flip(gathered, bit))
    gathered = jnp.concatenate(quarters, axis=0)
    for bit in reversed(bits[1:-2]):
        got_rows = flip(gathered, bit)
        gathered = jnp.concatenate([gathered, got_rows], axis=0)
    halves = (gathered, flip(gathered, bits[0]))

    def audio_spec(which):
        return pl.BlockSpec((half, wide), lambda step: (0, which * steps + step))

    vid_spec = pl.BlockSpec((vid_rows, wide), lambda step: (0, step))
    scalar_spec = pl.BlockSpec(memory_space=pltpu.SMEM)
    stat_spec = pl.BlockSpec((group, 8, rows), lambda step: (step, 0, 0))
    stat_shape = jax.ShapeDtypeStruct((pairs, 8, rows), F32)

    def part_spec(count):
        return pl.BlockSpec((count, half, wide), lambda step: (0, 0, step))

    def part_shapes(count, part_rows):
        return [
            jax.ShapeDtypeStruct((count, part_rows, width), F32),
            jax.ShapeDtypeStruct((count, part_rows, width), BF16),
        ]

    product = 2 * vid_rows * 2 * rows * PAIR * pairs
    vid_bytes = 2 * vid_rows * width
    vid_shape = jax.ShapeDtypeStruct((vid_rows, width), BF16)

    def cost(matmuls, moved):
        return pl.CostEstimate(
            flops=matmuls * product, bytes_accessed=moved * vid_bytes, transcendentals=vid_rows * 2 * rows * pairs
        )

    stats, keep_a, send_a = pl.pallas_call(
        audio_kernel,
        grid=(steps,),
        compiler_params=PARAMS,
        in_specs=[scalar_spec, audio_spec(0), audio_spec(0), audio_spec(3), audio_spec(3), vid_spec, vid_spec],
        out_specs=[stat_spec, part_spec(3), part_spec(3)],
        out_shape=[stat_shape, *part_shapes(3, half)],
        cost_estimate=cost(5, 5),
        name="audio_side",
    )(live, *halves, *halves, video_k, video_v)

    if head_size == 2:
        tok_spec = pl.BlockSpec((tok_rows, wide), lambda step: (0, step))
        out_specs = [tok_spec, tok_spec]
        out_shapes = [jax.ShapeDtypeStruct((tok_rows, width), BF16)] * 2
    else:
        out_specs, out_shapes = [vid_spec], [vid_shape]
    *attended, grad_video_q, keep_b, send_b = pl.pallas_call(
        video_kernel,
        grid=(steps,),
        compiler_params=PARAMS,
        in_specs=[scalar_spec, audio_spec(1), audio_spec(1), audio_spec(2), audio_spec(2), vid_spec, vid_spec],
        out_specs=[*out_specs, vid_spec, part_spec(2), part_spec(2)],
        out_shape=[*out_shapes, vid_shape, *part_shapes(2, half)],
        cost_estimate=cost(6, 6),
        name="video_side",
    )(head_index.astype(jnp.int32)[None], *halves, *halves, video_q, video_grad)

    if head_size == 2:
        mine, theirs = attended
        other = lax.ppermute(theirs, "head", [(0, 1), (1, 0)])
        video_out = jnp.concatenate(
            [jnp.where(head_index == 0, mine, other), jnp.where(head_index == 0, other, mine)], axis=1
        )[None]
    else:
        video_out = lax.all_to_all(attended[0], "head", split_axis=0, concat_axis=1, tiled=True)[None]

    levels = [stats]
    others = []
    shift = half
    for bit in bits:
        others.append(flip(levels[-1], bit))
        levels.append(
            pl.pallas_call(
                functools.partial(stats_kernel, shift), out_shape=stat_shape, compiler_params=PARAMS
            )(levels[-1], others[-1])
        )
        shift //= 2

    keeps, sends = (keep_a, keep_b), (send_a, send_b)
    part_rows = half
    for level, bit in enumerate(bits[:-2]):
        recvs = []
        for send in sends:
            recvs.append(flip(send, bit))
        if level < len(bits) - 3:
            keep, send = pl.pallas_call(
                functools.partial(merge_kernel, len(keeps), part_rows),
                out_shape=part_shapes(5, part_rows // 2),
                compiler_params=PARAMS,
            )(levels[level], others[level], *keeps, *recvs)
            keeps, sends = (keep,), (send,)
            part_rows //= 2
        else:
            slots = pl.pallas_call(
                functools.partial(settle_kernel, len(keeps), part_rows),
                out_shape=[jax.ShapeDtypeStruct((4, aud_rows, width), dtype) for dtype in (F32, BF16, BF16, BF16)],
                compiler_params=PARAMS,
                name="settle",
            )(levels[level], others[level], levels[-1], *keeps, *recvs)
    high, low = bits[-1], bits[-2]
    parts = [slots[0]]
    for bit, slot in zip((high, low, high | low), slots[1:]):
        parts.append(flip(slot, bit))
    audio_out, grad_audio_q, grad_audio_k, grad_audio_v = pl.pallas_call(
        add_kernel,
        out_shape=[jax.ShapeDtypeStruct((aud_rows, width), BF16)] * 4,
        compiler_params=PARAMS,
        name="add",
    )(*parts)

    grad_video_k, grad_video_v = pl.pallas_call(
        final_kernel,
        grid=(steps,),
        compiler_params=PARAMS,
        in_specs=[
            scalar_spec,
            audio_spec(0),
            audio_spec(0),
            audio_spec(3),
            audio_spec(3),
            vid_spec,
            vid_spec,
            stat_spec,
        ],
        out_specs=[vid_spec, vid_spec],
        out_shape=[vid_shape, vid_shape],
        cost_estimate=cost(4, 4),
        name="audio_grads",
    )(live, *halves, *halves, video_k, video_v, levels[-1])
    return (
        video_out,
        audio_out,
        grad_video_q,
        grad_video_k,
        grad_video_v,
        grad_audio_q,
        grad_audio_k,
        grad_audio_v,
    )


def solution(mesh):
    wide = P("ctx", "head")
    tall = P("ctx", "head", None)

    return jax.shard_map(
        body,
        mesh=mesh,
        in_specs=(wide, wide, wide, wide, wide, wide, P(), tall, wide),
        out_specs=(tall, wide, wide, wide, wide, wide, wide, wide),
        check_vma=False,
    )
```

time: 98.5 us -> 75.6 us (0.77); the launches traced: 96.9 us -> 75.1 us
  Pallas kernels: 33.6 us -> 17.9 us
  waiting for transfers between devices: 34.6 us -> 28.3 us
  starting transfers between devices: 18.8 us -> 22.4 us
  local copies, waits for them, and re-layouts: 6.47 us -> 3.94 us
    pallas_call x7 -> x11, Pallas kernels: 33.6 us -> 17.9 us  [the longest x1 7.46 us: body(): pl.pallas_call(video_kernel, grid=(steps,), compiler_params=PARAMS, in_sp...]
    ppermute x13 -> x15, waiting for transfers between devices: 28.3 us -> 21.8 us  [flip(): return lax.ppermute(x, 'ctx', [(i, i ^ bit) for i in range(ctx_size)])]
    ppermute x13 -> x15, starting transfers between devices: 15.4 us -> 19.3 us  [flip(): return lax.ppermute(x, 'ctx', [(i, i ^ bit) for i in range(ctx_size)])]
    unnamed x39 -> x20, local copies, waits for them, and re-layouts: 6.43 us -> 3.9 us
  transfers between devices with their start and end apart: 15 -> 17, of which waited for: 9 -> 11; matrix products, arithmetic and copies ran while one was open for 2% -> 1% of each run, Pallas kernels for 19% -> 17%
where the time goes in v2:
time: 75.6 us; the launch traced here: 75.1 us
  waiting for transfers between devices  28.3 us (37%)
  starting transfers between devices  22.4 us (30%)
  Pallas kernels  17.9 us (24%)
  local copies, waits for them, and re-layouts  3.94 us (5%)
  between operations  1.5 us (2%)
  other arithmetic  1.05 us (1%)
    ppermute x15, waiting for transfers between devices, flip(): return lax.ppermute(x, 'ctx', [(i, i ^ bit) for i in range(ctx_size)])  21.8 us
    ppermute x15, starting transfers between devices, flip(): return lax.ppermute(x, 'ctx', [(i, i ^ bit) for i in range(ctx_size)])  19.3 us
    pallas_call x1, Pallas kernels, body(): pl.pallas_call(video_kernel, grid=(steps,), compiler_params=PARAMS, in_sp...  7.46 us
    ppermute x1, waiting for transfers between devices, body(): got = lax.ppermute(sent, 'head', [(0, 1), (1, 0)])  6.48 us
    pallas_call x1, Pallas kernels, body(): pl.pallas_call(audio_kernel, grid=(steps,), compiler_params=PARAMS, in_sp...  4.15 us
    unnamed x20, local copies, waits for them, and re-layouts  3.9 us
    pallas_call x1, Pallas kernels, body(): pl.pallas_call(final_kernel, grid=(steps,), compiler_params=PARAMS, in_sp...  3.67 us
    ppermute x1, starting transfers between devices, body(): got = lax.ppermute(sent, 'head', [(0, 1), (1, 0)])  1.58 us
  transfers between devices with their start and end apart: 17, of which 11 were waited for; matrix products, arithmetic and copies ran while one was open for 1% of the time, Pallas kernels for 17%

profile of v2, /device:TPU:0, one launch (start us, length us, event | category | flops | bytes accessed | tf_op | source)
XLA Modules:
  0.0 75.1 jit_solution(13171253548660526323)
XLA Ops:
  0.6 0.7 copy-done.3
  1.4 0.7 copy-done.4
  2.1 0.7 copy-done.5
  2.8 0.7 copy-done.6
  3.5 4.1 %collective-permute-start = (bf16[8,4096]{1,0:T(8,128)(2,1)S(1)}, bf16[8,4096]{1,0:T(8,128)(2,1)S(1)}, u32[]{:S(2)}, u32[]{:S(2)}) collective-permute-start(bf16[8,4096]{1,0:T(8,128)(2,1)S(1)} %pack.1), channel_id=1, source_target_pairs={{0,8},{1,9},{2,10},{3,11},{4,12},{5,13},{6,14},{7,15},{8,0},{9,1},... | collective-permute-start | bytes 196616 | tf_op jit(solution)/shard_map/ppermute | solution.py:284
  7.6 1.6 %collective-permute-start.1 = (bf16[8,4096]{1,0:T(8,128)(2,1)S(1)}, bf16[8,4096]{1,0:T(8,128)(2,1)S(1)}, u32[]{:S(2)}, u32[]{:S(2)}) collective-permute-start(bf16[8,4096]{1,0:T(8,128)(2,1)S(1)} %pack.1), channel_id=1, source_target_pairs={{0,4},{1,5},{2,6},{3,7},{4,0},{5,1},{6,2},{7,3},{8,12},{9,13},{10,... | collective-permute-start | bytes 196616 | tf_op jit(solution)/shard_map/ppermute | solution.py:284
  9.2 1.5 %collective-permute-done = bf16[8,4096]{1,0:T(8,128)(2,1)S(1)} collective-permute-done((bf16[8,4096]{1,0:T(8,128)(2,1)S(1)}, bf16[8,4096]{1,0:T(8,128)(2,1)S(1)}, u32[]{:S(2)}, u32[]{:S(2)}) %collective-permute-start) | collective-permute-done | bytes 65568 | tf_op jit(solution)/shard_map/ppermute | solution.py:284
  10.6 1.2 %collective-permute-done.1 = bf16[8,4096]{1,0:T(8,128)(2,1)S(1)} collective-permute-done((bf16[8,4096]{1,0:T(8,128)(2,1)S(1)}, bf16[8,4096]{1,0:T(8,128)(2,1)S(1)}, u32[]{:S(2)}, u32[]{:S(2)}) %collective-permute-start.1) | collective-permute-done | bytes 65568 | tf_op jit(solution)/shard_map/ppermute | solution.py:284
  11.8 3.4 %collective-permute-done.2 = bf16[8,4096]{1,0:T(8,128)(2,1)S(1)} collective-permute-done((bf16[8,4096]{1,0:T(8,128)(2,1)S(1)}, bf16[8,4096]{1,0:T(8,128)(2,1)S(1)}, u32[]{:S(2)}, u32[]{:S(2)}) %collective-permute-start.2) | collective-permute-done | bytes 65568 | tf_op jit(solution)/shard_map/ppermute | solution.py:284
  15.2 0.0 copy-start.7
  15.3 1.6 %collective-permute-start.3 = (bf16[32,4096]{1,0:T(8,128)(2,1)S(1)}, bf16[32,4096]{1,0:T(8,128)(2,1)S(1)}, u32[]{:S(2)}, u32[]{:S(2)}) collective-permute-start(bf16[32,4096]{1,0:T(8,128)(2,1)S(1)} %pad_maximum_fusion.1), channel_id=1, source_target_pairs={{0,2},{1,3},{2,0},{3,1},{4,6},{5,7},{6,4},{7,5},{8,10},{9,11},{10,... | collective-permute-start | bytes 786440 | tf_op jit(solution)/shard_map/ppermute | solution.py:284
  16.8 4.9 %collective-permute-done.3 = bf16[32,4096]{1,0:T(8,128)(2,1)S(1)} collective-permute-done((bf16[32,4096]{1,0:T(8,128)(2,1)S(1)}, bf16[32,4096]{1,0:T(8,128)(2,1)S(1)}, u32[]{:S(2)}, u32[]{:S(2)}) %collective-permute-start.3) | collective-permute-done | bytes 262176 | tf_op jit(solution)/shard_map/ppermute | solution.py:284
  21.8 0.1 collective-permute-start.4
  21.9 1.6 %collective-permute-start.5 = (bf16[128,1024]{1,0:T(8,128)(2,1)S(1)}, bf16[128,1024]{1,0:T(8,128)(2,1)S(1)}, u32[]{:S(2)}, u32[]{:S(2)}) collective-permute-start(bf16[128,1024]{1,0:T(8,128)(2,1)S(1)} %dynamic-slice_bitcast_fusion), channel_id=1, source_target_pairs={{0,16},{16,0},{1,17},{17,1},{2,18},{18,2},{3,19},{19,3},{4,20},{20... | collective-permute-start | bytes 786440 | tf_op jit(solution)/shard_map/ppermute | solution.py:291
  24.1 0.0 copy-start
  24.2 0.0 copy-start.1
  24.2 6.5 %collective-permute-done.5 = bf16[128,1024]{1,0:T(8,128)(2,1)S(1)} collective-permute-done((bf16[128,1024]{1,0:T(8,128)(2,1)S(1)}, bf16[128,1024]{1,0:T(8,128)(2,1)S(1)}, u32[]{:S(2)}, u32[]{:S(2)}) %collective-permute-start.5) | collective-permute-done | bytes 262176 | tf_op jit(solution)/shard_map/ppermute | solution.py:291
  30.7 0.1 bitcast_select_fusion.1
  30.8 4.1 %audio_side.1 = (f32[8,8,128]{2,1,0:T(8,128)S(1)}, f32[3,64,1024]{2,1,0:T(8,128)S(1)}, bf16[3,64,1024]{2,1,0:T(8,128)(2,1)S(1)}) custom-call(s32[1]{0:T(128)S(6)} %min.6.live_ref, bf16[64,4096]{1,0:T(8,128)(2,1)S(1)} %constant_dynamic-update-slice_fusion.k_lo.v_lo.q_lo.c_lo, bf16[64,4096]{1,0:T(8,128)(2,1)S(1)} %collective-permute-done.4.k_hi.v_hi.q_hi.c_hi, ...), custom_call_target="tpu_custom_call" | custom-call | flops 671088640 | bytes 2621440 | tf_op jit(solution)/shard_map/audio_side/pallas_call | solution.py:339
  34.9 0.1 collective-permute-start.11
  35.0 0.0 copy-start.2
  35.1 1.0 %copy-done.2 = bf16[256,1024]{1,0:T(8,128)(2,1)S(1)} copy-done((bf16[256,1024]{1,0:T(8,128)(2,1)S(1)}, bf16[256,1024]{1,0:T(8,128)(2,1)}, u32[]{:S(2)}) %copy-start.2) | copy-done | bytes 524312
  36.1 7.5 %video_side.1 = (bf16[128,1024]{1,0:T(8,128)(2,1)S(1)}, bf16[128,1024]{1,0:T(8,128)(2,1)S(1)}, bf16[256,1024]{1,0:T(8,128)(2,1)}, f32[2,64,1024]{2,1,0:T(8,128)S(1)}, bf16[2,64,1024]{2,1,0:T(8,128)(2,1)S(1)}) custom-call(s32[1]{0:T(128)} %bitcast.head_ref, bf16[64,4096]{1,0:T(8,128)(2,1)S(1)} %constant_dynamic-update-slice_fusion.k_lo.v_lo.q_lo.c_lo, ...), custom_call_target="tpu_custom_call" | custom-call | flops 805306368 | bytes 3145728 | tf_op jit(solution)/shard_map/video_side/pallas_call | solution.py:356
  43.5 0.5 collective-permute-start.12
  44.0 1.5 %collective-permute-start.6 = (bf16[128,1024]{1,0:T(8,128)(2,1)S(1)}, bf16[128,1024]{1,0:T(8,128)(2,1)S(1)}, u32[]{:S(2)}, u32[]{:S(2)}) collective-permute-start(bf16[128,1024]{1,0:T(8,128)(2,1)S(1)} %get-tuple-element.29), channel_id=1, source_target_pairs={{0,16},{16,0},{1,17},{17,1},{2,18},{18,2},{3,19},{19,3},{4,20},{20... | collective-permute-start | bytes 786440 | tf_op jit(solution)/shard_map/ppermute | solution.py:369
  45.6 1.2 %collective-permute-done.7.other_ref.refs_1_ = f32[8,8,128]{2,1,0:T(8,128)S(1)} collective-permute-done((f32[8,8,128]{2,1,0:T(8,128)S(1)}, f32[8,8,128]{2,1,0:T(8,128)S(1)}, u32[]{:S(2)}, u32[]{:S(2)}) %collective-permute-start.7) | collective-permute-done | bytes 32800 | tf_op jit(solution)/shard_map/ppermute | solution.py:284
  46.8 0.1 shard_map.152.mine_ref.refs_0_
  46.9 1.6 %collective-permute-start.8 = (f32[8,8,128]{2,1,0:T(8,128)S(1)}, f32[8,8,128]{2,1,0:T(8,128)S(1)}, u32[]{:S(2)}, u32[]{:S(2)}) collective-permute-start(f32[8,8,128]{2,1,0:T(8,128)S(1)} %shard_map.152.mine_ref.refs_0_), channel_id=1, source_target_pairs={{0,2},{1,3},{2,0},{3,1},{4,6},{5,7},{6,4},{7,5},{8,10},{9,11},{10,... | collective-permute-start | bytes 98312 | tf_op jit(solution)/shard_map/ppermute | solution.py:284
  48.4 2.4 %collective-permute-done.8.other_ref.refs_1_ = f32[8,8,128]{2,1,0:T(8,128)S(1)} collective-permute-done((f32[8,8,128]{2,1,0:T(8,128)S(1)}, f32[8,8,128]{2,1,0:T(8,128)S(1)}, u32[]{:S(2)}, u32[]{:S(2)}) %collective-permute-start.8) | collective-permute-done | bytes 32800 | tf_op jit(solution)/shard_map/ppermute | solution.py:284
  50.8 0.1 shard_map.153.mine_ref
  51.0 0.8 %collective-permute-start.9 = (f32[8,8,128]{2,1,0:T(8,128)S(1)}, f32[8,8,128]{2,1,0:T(8,128)S(1)}, u32[]{:S(2)}, u32[]{:S(2)}) collective-permute-start(f32[8,8,128]{2,1,0:T(8,128)S(1)} %shard_map.153.mine_ref), channel_id=1, source_target_pairs={{0,4},{1,5},{2,6},{3,7},{4,0},{5,1},{6,2},{7,3},{8,12},{9,13},{10,... | collective-permute-start | bytes 98312 | tf_op jit(solution)/shard_map/ppermute | solution.py:284
  51.7 3.2 %collective-permute-done.9.other_ref = f32[8,8,128]{2,1,0:T(8,128)S(1)} collective-permute-done((f32[8,8,128]{2,1,0:T(8,128)S(1)}, f32[8,8,128]{2,1,0:T(8,128)S(1)}, u32[]{:S(2)}, u32[]{:S(2)}) %collective-permute-start.9) | collective-permute-done | bytes 32800 | tf_op jit(solution)/shard_map/ppermute | solution.py:284
  54.9 0.1 shard_map.154.mine_ref
  55.1 3.1 %collective-permute-start.10 = (f32[8,8,128]{2,1,0:T(8,128)S(1)}, f32[8,8,128]{2,1,0:T(8,128)S(1)}, u32[]{:S(2)}, u32[]{:S(2)}) collective-permute-start(f32[8,8,128]{2,1,0:T(8,128)S(1)} %shard_map.154.mine_ref), channel_id=1, source_target_pairs={{0,8},{1,9},{2,10},{3,11},{4,12},{5,13},{6,14},{7,15},{8,0},{9,1},... | collective-permute-start | bytes 98312 | tf_op jit(solution)/shard_map/ppermute | solution.py:284
  58.1 0.9 %shard_map.156 = (f32[5,32,1024]{2,1,0:T(8,128)S(1)}, bf16[5,32,1024]{2,1,0:T(8,128)(2,1)S(1)}) custom-call(f32[8,8,128]{2,1,0:T(8,128)S(1)} %get-tuple-element.30.mine_ref.refs_0_, f32[8,8,128]{2,1,0:T(8,128)S(1)} %collective-permute-done.7.other_ref.refs_1_, f32[3,64,1024]{2,1,0:T(8,128)S(1)} %get-tuple-element.31.refs_2_, ...), custom_call_target="tpu_custom_call" | custom-call | tf_op jit(solution)/shard_map/pallas_call | solution.py:395
  59.1 1.6 %collective-permute-start.13 = (bf16[5,32,1024]{2,1,0:T(8,128)(2,1)S(1)}, bf16[5,32,1024]{2,1,0:T(8,128)(2,1)S(1)}, u32[]{:S(2)}, u32[]{:S(2)}) collective-permute-start(bf16[5,32,1024]{2,1,0:T(8,128)(2,1)S(1)} %get-tuple-element.36), channel_id=1, source_target_pairs={{0,2},{1,3},{2,0},{3,1},{4,6},{5,7},{6,4},{7,5},{8,10},{9,11},{10,... | collective-permute-start | bytes 983048 | tf_op jit(solution)/shard_map/ppermute | solution.py:284
  60.7 0.1 shard_map.155.refs_2_.stat_ref
  60.8 3.7 %audio_grads.1 = (bf16[256,1024]{1,0:T(8,128)(2,1)}, bf16[256,1024]{1,0:T(8,128)(2,1)}) custom-call(s32[1]{0:T(128)S(6)} %min.6.live_ref, bf16[64,4096]{1,0:T(8,128)(2,1)S(1)} %constant_dynamic-update-slice_fusion.k_lo.v_lo.q_lo.c_lo, bf16[64,4096]{1,0:T(8,128)(2,1)S(1)} %collective-permute-done.4.k_hi.v_hi.q_hi.c_hi, ...), custom_call_target="tpu_custom_call" | custom-call | flops 536870912 | bytes 2097152 | tf_op jit(solution)/shard_map/audio_grads/pallas_call | solution.py:420
  64.5 0.1 broadcast_select_fusion.1
  64.5 1.9 %collective-permute-done.13.refs_4_ = bf16[5,32,1024]{2,1,0:T(8,128)(2,1)S(1)} collective-permute-done((bf16[5,32,1024]{2,1,0:T(8,128)(2,1)S(1)}, bf16[5,32,1024]{2,1,0:T(8,128)(2,1)S(1)}, u32[]{:S(2)}, u32[]{:S(2)}) %collective-permute-start.13) | collective-permute-done | bytes 327712 | tf_op jit(solution)/shard_map/ppermute | solution.py:284
  66.4 0.6 settle.1
  67.0 0.5 collective-permute-start.14
  67.5 0.5 collective-permute-start.15
  68.0 3.5 %collective-permute-start.16 = (bf16[4,8,1024]{2,1,0:T(8,128)(2,1)S(1)}, bf16[4,8,1024]{2,1,0:T(8,128)(2,1)S(1)}, u32[]{:S(2)}, u32[]{:S(2)}) collective-permute-start(bf16[4,8,1024]{2,1,0:T(8,128)(2,1)S(1)} %get-tuple-element.40), channel_id=1, source_target_pairs={{0,12},{1,13},{2,14},{3,15},{4,8},{5,9},{6,10},{7,11},{8,4},{9,5},... | collective-permute-start | bytes 196616 | tf_op jit(solution)/shard_map/ppermute | solution.py:284
  71.5 0.8 %maximum_bitcast_fusion = bf16[1,128,2048]{2,1,0:T(8,128)(2,1)} fusion(bf16[128,1024]{1,0:T(8,128)(2,1)S(1)} %get-tuple-element.51, bf16[128,1024]{1,0:T(8,128)(2,1)S(1)} %get-tuple-element.50), kind=kLoop, calls=%fused_computation.1 | loop fusion | flops 1048576 | bytes 1048576 | tf_op jit(solution)/shard_map/broadcast_in_dim | solution.py:370
  72.3 0.4 collective-permute-done.14.refs_1_
  72.7 1.7 %collective-permute-done.16.refs_3_ = bf16[4,8,1024]{2,1,0:T(8,128)(2,1)S(1)} collective-permute-done((bf16[4,8,1024]{2,1,0:T(8,128)(2,1)S(1)}, bf16[4,8,1024]{2,1,0:T(8,128)(2,1)S(1)}, u32[]{:S(2)}, u32[]{:S(2)}) %collective-permute-start.16) | collective-permute-done | bytes 65568 | tf_op jit(solution)/shard_map/ppermute | solution.py:284
  74.4 0.6 add.9
  (24 shorter events, 0.2 us)
Async XLA Ops:
  0.6 0.7 copy-start.3
  1.4 0.7 copy-start.4
  2.1 0.7 copy-start.5
  2.8 0.7 copy-start.6
  3.5 7.1 %collective-permute-start = (bf16[8,4096]{1,0:T(8,128)(2,1)S(1)}, bf16[8,4096]{1,0:T(8,128)(2,1)S(1)}, u32[]{:S(2)}, u32[]{:S(2)}) collective-permute-start(bf16[8,4096]{1,0:T(8,128)(2,1)S(1)} %pack.1), channel_id=1, source_target_pairs={{0,8},{1,9},{2,10},{3,11},{4,12},{5,13},{6,14},{7,15},{8,0},{9,1},... | collective-permute-start | bytes 196616 | tf_op jit(solution)/shard_map/ppermute | solution.py:284
  7.6 4.3 %collective-permute-start.1 = (bf16[8,4096]{1,0:T(8,128)(2,1)S(1)}, bf16[8,4096]{1,0:T(8,128)(2,1)S(1)}, u32[]{:S(2)}, u32[]{:S(2)}) collective-permute-start(bf16[8,4096]{1,0:T(8,128)(2,1)S(1)} %pack.1), channel_id=1, source_target_pairs={{0,4},{1,5},{2,6},{3,7},{4,0},{5,1},{6,2},{7,3},{8,12},{9,13},{10,... | collective-permute-start | bytes 196616 | tf_op jit(solution)/shard_map/ppermute | solution.py:284
  9.2 6.1 %collective-permute-start.2 = (bf16[8,4096]{1,0:T(8,128)(2,1)S(1)}, bf16[8,4096]{1,0:T(8,128)(2,1)S(1)}, u32[]{:S(2)}, u32[]{:S(2)}) collective-permute-start(bf16[8,4096]{1,0:T(8,128)(2,1)S(1)} %pack.1), channel_id=1, source_target_pairs={{0,12},{1,13},{2,14},{3,15},{4,8},{5,9},{6,10},{7,11},{8,4},{9,5},... | collective-permute-start | bytes 196616 | tf_op jit(solution)/shard_map/ppermute | solution.py:284
  15.2 6.6 %copy-start.7 = (bf16[1,128,2048]{2,1,0:T(8,128)(2,1)S(1)}, bf16[1,128,2048]{2,1,0:T(8,128)(2,1)}, u32[]{:S(2)}) copy-start(bf16[1,128,2048]{2,1,0:T(8,128)(2,1)} %param.16) | copy-start | bytes 1572868
  15.3 6.5 %collective-permute-start.3 = (bf16[32,4096]{1,0:T(8,128)(2,1)S(1)}, bf16[32,4096]{1,0:T(8,128)(2,1)S(1)}, u32[]{:S(2)}, u32[]{:S(2)}) collective-permute-start(bf16[32,4096]{1,0:T(8,128)(2,1)S(1)} %pad_maximum_fusion.1), channel_id=1, source_target_pairs={{0,2},{1,3},{2,0},{3,1},{4,6},{5,7},{6,4},{7,5},{8,10},{9,11},{10,... | collective-permute-start | bytes 786440 | tf_op jit(solution)/shard_map/ppermute | solution.py:284
  21.8 9.0 %collective-permute-start.4 = (bf16[64,4096]{1,0:T(8,128)(2,1)S(1)}, bf16[64,4096]{1,0:T(8,128)(2,1)S(1)}, u32[]{:S(2)}, u32[]{:S(2)}) collective-permute-start(bf16[64,4096]{1,0:T(8,128)(2,1)S(1)} %constant_dynamic-update-slice_fusion.k_lo.v_lo.q_lo.c_lo), channel_id=1, source_target_pairs={{0,1},{1,0},{2,3},{3,2},{4,5},{5,4},{6,7},{7,6},{8,9},{9,8},{10,11... | collective-permute-start | bytes 1572872 | tf_op jit(solution)/shard_map/ppermute | solution.py:284
  21.9 8.8 %collective-permute-start.5 = (bf16[128,1024]{1,0:T(8,128)(2,1)S(1)}, bf16[128,1024]{1,0:T(8,128)(2,1)S(1)}, u32[]{:S(2)}, u32[]{:S(2)}) collective-permute-start(bf16[128,1024]{1,0:T(8,128)(2,1)S(1)} %dynamic-slice_bitcast_fusion), channel_id=1, source_target_pairs={{0,16},{16,0},{1,17},{17,1},{2,18},{18,2},{3,19},{19,3},{4,20},{20... | collective-permute-start | bytes 786440 | tf_op jit(solution)/shard_map/ppermute | solution.py:291
  24.1 6.6 %copy-start = (bf16[256,1024]{1,0:T(8,128)(2,1)S(1)}, bf16[256,1024]{1,0:T(8,128)(2,1)}, u32[]{:S(2)}) copy-start(bf16[256,1024]{1,0:T(8,128)(2,1)} %key_ref.3) | copy-start | bytes 1572868
  24.2 6.6 %copy-start.1 = (bf16[256,1024]{1,0:T(8,128)(2,1)S(1)}, bf16[256,1024]{1,0:T(8,128)(2,1)}, u32[]{:S(2)}) copy-start(bf16[256,1024]{1,0:T(8,128)(2,1)} %val_ref.3) | copy-start | bytes 1572868
  34.9 23.2 %collective-permute-start.11 = (bf16[3,64,1024]{2,1,0:T(8,128)(2,1)S(1)}, bf16[3,64,1024]{2,1,0:T(8,128)(2,1)S(1)}, u32[]{:S(2)}, u32[]{:S(2)}) collective-permute-start(bf16[3,64,1024]{2,1,0:T(8,128)(2,1)S(1)} %get-tuple-element.33), channel_id=1, source_target_pairs={{0,1},{1,0},{2,3},{3,2},{4,5},{5,4},{6,7},{7,6},{8,9},{9,8},{10,11... | collective-permute-start | bytes 1179656 | tf_op jit(solution)/shard_map/ppermute | solution.py:284
  35.0 1.0 %copy-start.2 = (bf16[256,1024]{1,0:T(8,128)(2,1)S(1)}, bf16[256,1024]{1,0:T(8,128)(2,1)}, u32[]{:S(2)}) copy-start(bf16[256,1024]{1,0:T(8,128)(2,1)} %query_ref.1) | copy-start | bytes 1572868
  43.5 14.6 %collective-permute-start.12 = (bf16[2,64,1024]{2,1,0:T(8,128)(2,1)S(1)}, bf16[2,64,1024]{2,1,0:T(8,128)(2,1)S(1)}, u32[]{:S(2)}, u32[]{:S(2)}) collective-permute-start(bf16[2,64,1024]{2,1,0:T(8,128)(2,1)S(1)} %get-tuple-element.34), channel_id=1, source_target_pairs={{0,1},{1,0},{2,3},{3,2},{4,5},{5,4},{6,7},{7,6},{8,9},{9,8},{10,11... | collective-permute-start | bytes 786440 | tf_op jit(solution)/shard_map/ppermute | solution.py:284
  44.0 20.4 %collective-permute-start.6 = (bf16[128,1024]{1,0:T(8,128)(2,1)S(1)}, bf16[128,1024]{1,0:T(8,128)(2,1)S(1)}, u32[]{:S(2)}, u32[]{:S(2)}) collective-permute-start(bf16[128,1024]{1,0:T(8,128)(2,1)S(1)} %get-tuple-element.29), channel_id=1, source_target_pairs={{0,16},{16,0},{1,17},{17,1},{2,18},{18,2},{3,19},{19,3},{4,20},{20... | collective-permute-start | bytes 786440 | tf_op jit(solution)/shard_map/ppermute | solution.py:369
  45.6 1.2 %collective-permute-start.7 = (f32[8,8,128]{2,1,0:T(8,128)S(1)}, f32[8,8,128]{2,1,0:T(8,128)S(1)}, u32[]{:S(2)}, u32[]{:S(2)}) collective-permute-start(f32[8,8,128]{2,1,0:T(8,128)S(1)} %get-tuple-element.30.mine_ref.refs_0_), channel_id=1, source_target_pairs={{0,1},{1,0},{2,3},{3,2},{4,5},{5,4},{6,7},{7,6},{8,9},{9,8},{10,11... | collective-permute-start | bytes 98312 | tf_op jit(solution)/shard_map/ppermute | solution.py:284
  46.9 4.0 %collective-permute-start.8 = (f32[8,8,128]{2,1,0:T(8,128)S(1)}, f32[8,8,128]{2,1,0:T(8,128)S(1)}, u32[]{:S(2)}, u32[]{:S(2)}) collective-permute-start(f32[8,8,128]{2,1,0:T(8,128)S(1)} %shard_map.152.mine_ref.refs_0_), channel_id=1, source_target_pairs={{0,2},{1,3},{2,0},{3,1},{4,6},{5,7},{6,4},{7,5},{8,10},{9,11},{10,... | collective-permute-start | bytes 98312 | tf_op jit(solution)/shard_map/ppermute | solution.py:284
  51.0 4.0 %collective-permute-start.9 = (f32[8,8,128]{2,1,0:T(8,128)S(1)}, f32[8,8,128]{2,1,0:T(8,128)S(1)}, u32[]{:S(2)}, u32[]{:S(2)}) collective-permute-start(f32[8,8,128]{2,1,0:T(8,128)S(1)} %shard_map.153.mine_ref), channel_id=1, source_target_pairs={{0,4},{1,5},{2,6},{3,7},{4,0},{5,1},{6,2},{7,3},{8,12},{9,13},{10,... | collective-permute-start | bytes 98312 | tf_op jit(solution)/shard_map/ppermute | solution.py:284
  55.1 5.6 %collective-permute-start.10 = (f32[8,8,128]{2,1,0:T(8,128)S(1)}, f32[8,8,128]{2,1,0:T(8,128)S(1)}, u32[]{:S(2)}, u32[]{:S(2)}) collective-permute-start(f32[8,8,128]{2,1,0:T(8,128)S(1)} %shard_map.154.mine_ref), channel_id=1, source_target_pairs={{0,8},{1,9},{2,10},{3,11},{4,12},{5,13},{6,14},{7,15},{8,0},{9,1},... | collective-permute-start | bytes 98312 | tf_op jit(solution)/shard_map/ppermute | solution.py:284
  59.1 7.3 %collective-permute-start.13 = (bf16[5,32,1024]{2,1,0:T(8,128)(2,1)S(1)}, bf16[5,32,1024]{2,1,0:T(8,128)(2,1)S(1)}, u32[]{:S(2)}, u32[]{:S(2)}) collective-permute-start(bf16[5,32,1024]{2,1,0:T(8,128)(2,1)S(1)} %get-tuple-element.36), channel_id=1, source_target_pairs={{0,2},{1,3},{2,0},{3,1},{4,6},{5,7},{6,4},{7,5},{8,10},{9,11},{10,... | collective-permute-start | bytes 983048 | tf_op jit(solution)/shard_map/ppermute | solution.py:284
  67.0 5.7 %collective-permute-start.14 = (bf16[4,8,1024]{2,1,0:T(8,128)(2,1)S(1)}, bf16[4,8,1024]{2,1,0:T(8,128)(2,1)S(1)}, u32[]{:S(2)}, u32[]{:S(2)}) collective-permute-start(bf16[4,8,1024]{2,1,0:T(8,128)(2,1)S(1)} %get-tuple-element.38), channel_id=1, source_target_pairs={{0,8},{1,9},{2,10},{3,11},{4,12},{5,13},{6,14},{7,15},{8,0},{9,1},... | collective-permute-start | bytes 196616 | tf_op jit(solution)/shard_map/ppermute | solution.py:284
  67.5 5.2 %collective-permute-start.15 = (bf16[4,8,1024]{2,1,0:T(8,128)(2,1)S(1)}, bf16[4,8,1024]{2,1,0:T(8,128)(2,1)S(1)}, u32[]{:S(2)}, u32[]{:S(2)}) collective-permute-start(bf16[4,8,1024]{2,1,0:T(8,128)(2,1)S(1)} %get-tuple-element.39), channel_id=1, source_target_pairs={{0,4},{1,5},{2,6},{3,7},{4,0},{5,1},{6,2},{7,3},{8,12},{9,13},{10,... | collective-permute-start | bytes 196616 | tf_op jit(solution)/shard_map/ppermute | solution.py:284
  68.0 6.5 %collective-permute-start.16 = (bf16[4,8,1024]{2,1,0:T(8,128)(2,1)S(1)}, bf16[4,8,1024]{2,1,0:T(8,128)(2,1)S(1)}, u32[]{:S(2)}, u32[]{:S(2)}) collective-permute-start(bf16[4,8,1024]{2,1,0:T(8,128)(2,1)S(1)} %get-tuple-element.40), channel_id=1, source_target_pairs={{0,12},{1,13},{2,14},{3,15},{4,8},{5,9},{6,10},{7,11},{8,4},{9,5},... | collective-permute-start | bytes 196616 | tf_op jit(solution)/shard_map/ppermute | solution.py:284

commit v3 on v2

--- a/solution.py
+++ b/solution.py
@@ -12,7 +12,7 @@
 PAIR = 2 * HEAD_DIM
 SCALE = HEAD_DIM ** (-0.5)
 NEG = -1e30
-GROUP = 2
+GROUP = 4
 PARAMS = pltpu.CompilerParams(vmem_limit_bytes=12 * 1024 * 1024)
 F32 = jnp.float32
 BF16 = jnp.bfloat16
@@ -24,10 +24,6 @@
 
 def nn(x, y):
     return jnp.dot(x, y, preferred_element_type=F32)
-
-
-def tn(x, y):
-    return lax.dot_general(x, y, (((0,), (0,)), ((), ())), preferred_element_type=F32)
 
 
 def first_head(shape):
@@ -83,6 +79,13 @@
         stat_ref[pair] = table.T[:8]
 
 
+def transposed_diag(low, high):
+    turned = jnp.concatenate([low, high], axis=0).T
+    keep = lax.broadcasted_iota(jnp.int32, turned.shape, 0) < HEAD_DIM
+    zero = jnp.zeros_like(turned)
+    return jnp.concatenate([jnp.where(keep, turned, zero), jnp.where(keep, zero, turned)], axis=1)
+
+
 def video_kernel(head_ref, k_lo, k_hi, v_lo, v_hi, query_ref, grad_ref, *outs):
     *out_refs, dq_ref, keep_ref, send_ref = outs
     for pair in range(query_ref.shape[1] // PAIR):
@@ -91,38 +94,30 @@
         keys = block_diag(k_lo[:, cols], k_hi[:, cols])
         vals = block_diag(v_lo[:, cols], v_hi[:, cols])
         rows = keys.shape[0] // 2
-        scores = nt(queries, keys) * SCALE
-        probs = []
-        for part in (scores[:, :rows], scores[:, rows:]):
-            shifted = jnp.exp(part - jnp.max(part, axis=1, keepdims=True))
-            probs.append(shifted * (1.0 / jnp.sum(shifted, axis=1, keepdims=True)))
-        rounded = jnp.concatenate([prob.astype(BF16) for prob in probs], axis=1)
-        attended = nn(rounded, vals)
+        scores = nt(keys, queries) * SCALE
+        dprob = nt(vals, grads)
+        probs, steps = [], []
+        for head in range(2):
+            span = slice(head * rows, (head + 1) * rows)
+            part, dpart = scores[span], dprob[span]
+            shifted = jnp.exp(part - jnp.max(part, axis=0, keepdims=True))
+            prob = shifted * (1.0 / jnp.sum(shifted, axis=0, keepdims=True))
+            proj = jnp.sum(prob * dpart, axis=0, keepdims=True)
+            probs.append(prob.astype(BF16))
+            steps.append((SCALE * prob * (dpart - proj)).astype(BF16))
+        rounded, step = jnp.concatenate(probs, axis=0), jnp.concatenate(steps, axis=0)
+        attended = nn(transposed_diag(v_lo[:, cols], v_hi[:, cols]), rounded).astype(BF16).T
         if len(out_refs) == 1:
-            out_refs[0][:, cols] = attended.astype(BF16)
+            out_refs[0][:, cols] = attended
         else:
             tok_rows = attended.shape[0] // 2
-            upper, lower = attended[:tok_rows].astype(BF16), attended[tok_rows:].astype(BF16)
+            upper, lower = attended[:tok_rows], attended[tok_rows:]
             is_first = jnp.full(upper.shape, head_ref[0], jnp.int32) == 0
             out_refs[0][:, cols] = jnp.where(is_first, upper, lower)
             out_refs[1][:, cols] = jnp.where(is_first, lower, upper)
-        dprob = nt(grads, vals)
-        product = grads.astype(F32) * attended
-        low = first_head(product.shape)
-        proj = (
-            jnp.sum(jnp.where(low, product, 0.0), axis=1, keepdims=True),
-            jnp.sum(jnp.where(low, 0.0, product), axis=1, keepdims=True),
-        )
-        steps = jnp.concatenate(
-            [
-                (SCALE * probs[h] * (dprob[:, h * rows : (h + 1) * rows] - proj[h])).astype(BF16)
-                for h in range(2)
-            ],
-            axis=1,
-        )
-        dq_ref[:, cols] = nn(steps, keys).astype(BF16)
+        dq_ref[:, cols] = nn(transposed_diag(k_lo[:, cols], k_hi[:, cols]), step).astype(BF16).T
         half = rows // 2
-        for index, part in enumerate((join_pair(tn(steps, queries)), join_pair(tn(rounded, grads)))):
+        for index, part in enumerate((join_pair(nn(step, queries)), join_pair(nn(rounded, grads)))):
             keep_ref[index, :, cols] = part[:half]
             send_ref[index, :, cols] = part[half:].astype(BF16)
 
@@ -159,55 +154,54 @@
     for pair in range(pairs):
         tables += factors(pair)
     table = jnp.concatenate(tables, axis=0)
-    if table.shape[0] < 128:
-        pad = jnp.zeros((128 - table.shape[0], table.shape[1]), F32)
+    if table.shape[0] % 128:
+        pad = jnp.zeros((-table.shape[0] % 128, table.shape[1]), F32)
         table = jnp.concatenate([table, pad], axis=0)
     return table.T
 
 
-def merged_parts(table, pair, keeps, recvs):
+def weigh(table, pair, rows):
+    low = first_head((rows, PAIR))
+    at = pair * 8
+    return [
+        jnp.where(low, table[:rows, col : col + 1], table[:rows, col + 1 : col + 2])
+        for col in (at, at + 2, at + 4, at + 6)
+    ]
+
+
+def audio_parts(table, pair, keep, recv):
     cols = pair_cols(pair)
-    rows = keeps[0].shape[1]
-    low = first_head((rows, PAIR))
-
-    def column(index):
-        at = pair * 8 + 2 * index
-        return jnp.where(low, table[:rows, at : at + 1], table[:rows, at + 1 : at + 2])
-
-    def fetch(group, index):
-        for ref in group:
-            if index < ref.shape[0]:
-                return ref[index, :, cols].astype(F32)
-            index -= ref.shape[0]
-
-    scale1, scale2, shift1, shift2 = (column(index) for index in range(4))
-    num1, step1, sum1, key1, val1 = (fetch(keeps, index) for index in range(5))
-    num2, step2, sum2, key2, val2 = (fetch(recvs, index) for index in range(5))
+    scale1, scale2, shift1, shift2 = weigh(table, pair, keep.shape[1])
+    num1, step1, sum1 = (keep[index, :, cols] for index in range(3))
+    num2, step2, sum2 = (recv[index, :, cols].astype(F32) for index in range(3))
     num = scale1 * num1 + scale2 * num2
     step = scale1 * step1 + shift1 * sum1 + scale2 * step2 + shift2 * sum2
-    return num, step, scale1 * sum1 + scale2 * sum2, key1 + key2, val1 + val2
-
-
-def merge_kernel(n_in, shift, *refs):
-    mine_ref, other_ref = refs[:2]
-    keeps, recvs = refs[2 : 2 + n_in], refs[2 + n_in : 2 + 2 * n_in]
-    keep_ref, send_ref = refs[2 + 2 * n_in :]
+    return num, step, scale1 * sum1 + scale2 * sum2
+
+
+def spread_rows(part, outs, index, cols):
+    rows = outs[0].shape[1]
+    for slot, out in enumerate(outs):
+        out[index, :, cols] = part[slot * rows : (slot + 1) * rows].astype(out.dtype)
+
+
+def merge_audio_kernel(shift, mine_ref, other_ref, keep, recv, *outs):
     pairs = mine_ref.shape[0]
-    half = keeps[0].shape[1] // 2
     table = merge_tables(
         pairs, lambda pair: list(merge_stats(mine_ref[pair], other_ref[pair], shift)[3:])
     )
     for pair in range(pairs):
         cols = pair_cols(pair)
-        for index, part in enumerate(merged_parts(table, pair, keeps, recvs)):
-            keep_ref[index, :, cols] = part[:half]
-            send_ref[index, :, cols] = part[half:].astype(BF16)
-
-
-def settle_kernel(n_in, shift, *refs):
-    mine_ref, other_ref, all_ref = refs[:3]
-    keeps, recvs = refs[3 : 3 + n_in], refs[3 + n_in : 3 + 2 * n_in]
-    outs = refs[3 + 2 * n_in :]
+        for index, part in enumerate(audio_parts(table, pair, keep, recv)):
+            spread_rows(part, outs, index, cols)
+
+
+def merge_video_kernel(keep, recv, *outs):
+    for index in range(2):
+        spread_rows(keep[index] + recv[index].astype(F32), outs, index, slice(None))
+
+
+def settle_kernel(shift, mine_ref, other_ref, all_ref, keep_a, recv_a, keep_b, recv_b, *outs):
     pairs = mine_ref.shape[0]
     rows = outs[0].shape[1]
 
@@ -223,7 +217,8 @@
     table = merge_tables(pairs, factors)
     for pair in range(pairs):
         cols = pair_cols(pair)
-        num, step, _, key, val = merged_parts(table, pair, keeps, recvs)
+        num, step, _ = audio_parts(table, pair, keep_a, recv_a)
+        key, val = (keep_b[index, :, cols] + recv_b[index, :, cols].astype(F32) for index in range(2))
         for index, part in enumerate((num, SCALE * step, key, val)):
             for slot, out in enumerate(outs):
                 out[index, :, cols] = part[slot * rows : (slot + 1) * rows].astype(out.dtype)
@@ -259,9 +254,16 @@
 
 
 def pack_kernel(*refs):
-    width = refs[0].shape[1]
-    for index, ref in enumerate(refs[:-1]):
-        refs[-1][:, index * width : (index + 1) * width] = ref[...]
+    *inputs, packed, sems = refs
+    width = inputs[0].shape[1]
+    copies = [
+        pltpu.make_async_copy(ref, packed.at[:, index * width : (index + 1) * width], sems.at[index])
+        for index, ref in enumerate(inputs)
+    ]
+    for copy in copies:
+        copy.start()
+    for copy in copies:
+        copy.wait()
 
 
 def body(video_q, video_k, video_v, audio_q, audio_k, audio_v, video_length, video_cot, audio_cot):
@@ -283,6 +285,8 @@
     def flip(x, bit):
         return lax.ppermute(x, "ctx", [(i, i ^ bit) for i in range(ctx_size)])
 
+    head_word = head_index.astype(jnp.int32)[None]
+    scalar_spec = pl.BlockSpec(memory_space=pltpu.SMEM)
     cot = video_cot[0]
     tok_rows = cot.shape[0]
     if head_size == 2:
@@ -297,8 +301,10 @@
 
     gathered = pl.pallas_call(
         pack_kernel,
+        in_specs=[pl.BlockSpec(memory_space=pltpu.HBM)] * 4,
+        out_specs=pl.BlockSpec(memory_space=pltpu.VMEM),
         out_shape=jax.ShapeDtypeStruct((aud_rows, 4 * width), BF16),
-        compiler_params=PARAMS,
+        scratch_shapes=[pltpu.SemaphoreType.DMA((4,))],
         name="pack",
     )(audio_q, audio_k, audio_v, audio_cot)
     quarters = [gathered]
@@ -314,7 +320,6 @@
         return pl.BlockSpec((half, wide), lambda step: (0, which * steps + step))
 
     vid_spec = pl.BlockSpec((vid_rows, wide), lambda step: (0, step))
-    scalar_spec = pl.BlockSpec(memory_space=pltpu.SMEM)
     stat_spec = pl.BlockSpec((group, 8, rows), lambda step: (step, 0, 0))
     stat_shape = jax.ShapeDtypeStruct((pairs, 8, rows), F32)
 
@@ -362,7 +367,7 @@
         out_shape=[*out_shapes, vid_shape, *part_shapes(2, half)],
         cost_estimate=cost(6, 6),
         name="video_side",
-    )(head_index.astype(jnp.int32)[None], *halves, *halves, video_q, video_grad)
+    )(head_word, *halves, *halves, video_q, video_grad)
 
     if head_size == 2:
         mine, theirs = attended
@@ -373,43 +378,43 @@
     else:
         video_out = lax.all_to_all(attended[0], "head", split_axis=0, concat_axis=1, tiled=True)[None]
 
-    levels = [stats]
-    others = []
-    shift = half
-    for bit in bits:
-        others.append(flip(levels[-1], bit))
-        levels.append(
-            pl.pallas_call(
-                functools.partial(stats_kernel, shift), out_shape=stat_shape, compiler_params=PARAMS
-            )(levels[-1], others[-1])
-        )
-        shift //= 2
-
-    keeps, sends = (keep_a, keep_b), (send_a, send_b)
     part_rows = half
+    high, low = bits[-1], bits[-2]
+    exchanges = tuple(zip((high, low, high | low), range(1, 4)))
     for level, bit in enumerate(bits[:-2]):
-        recvs = []
-        for send in sends:
-            recvs.append(flip(send, bit))
+        other = flip(stats, bit)
+        recv_a = flip(send_a, bit)
+        recv_b = flip(send_b, bit)
+        merged_stats = pl.pallas_call(
+            functools.partial(stats_kernel, part_rows), out_shape=stat_shape, compiler_params=PARAMS
+        )(stats, other)
         if level < len(bits) - 3:
-            keep, send = pl.pallas_call(
-                functools.partial(merge_kernel, len(keeps), part_rows),
-                out_shape=part_shapes(5, part_rows // 2),
+            keep_a, send_a = pl.pallas_call(
+                functools.partial(merge_audio_kernel, part_rows),
+                out_shape=part_shapes(3, part_rows // 2),
                 compiler_params=PARAMS,
-            )(levels[level], others[level], *keeps, *recvs)
-            keeps, sends = (keep,), (send,)
+            )(stats, other, keep_a, recv_a)
+            keep_b, send_b = pl.pallas_call(
+                merge_video_kernel, out_shape=part_shapes(2, part_rows // 2), compiler_params=PARAMS
+            )(keep_b, recv_b)
+            stats = merged_stats
             part_rows //= 2
         else:
+            final_stats = merged_stats
+            for step_bit, shift in ((low, 2 * aud_rows), (high, aud_rows)):
+                step_other = flip(final_stats, step_bit)
+                final_stats = pl.pallas_call(
+                    functools.partial(stats_kernel, shift), out_shape=stat_shape, compiler_params=PARAMS
+                )(final_stats, step_other)
             slots = pl.pallas_call(
-                functools.partial(settle_kernel, len(keeps), part_rows),
+                functools.partial(settle_kernel, part_rows),
                 out_shape=[jax.ShapeDtypeStruct((4, aud_rows, width), dtype) for dtype in (F32, BF16, BF16, BF16)],
                 compiler_params=PARAMS,
                 name="settle",
-            )(levels[level], others[level], levels[-1], *keeps, *recvs)
-    high, low = bits[-1], bits[-2]
+            )(stats, other, final_stats, keep_a, recv_a, keep_b, recv_b)
     parts = [slots[0]]
-    for bit, slot in zip((high, low, high | low), slots[1:]):
-        parts.append(flip(slot, bit))
+    for step_bit, slot in exchanges:
+        parts.append(flip(slots[slot], step_bit))
     audio_out, grad_audio_q, grad_audio_k, grad_audio_v = pl.pallas_call(
         add_kernel,
         out_shape=[jax.ShapeDtypeStruct((aud_rows, width), BF16)] * 4,
@@ -435,7 +440,7 @@
         out_shape=[vid_shape, vid_shape],
         cost_estimate=cost(4, 4),
         name="audio_grads",
-    )(live, *halves, *halves, video_k, video_v, levels[-1])
+    )(live, *halves, *halves, video_k, video_v, final_stats)
     return (
         video_out,
         audio_out,

time: 75.6 us -> 77.8 us (1.029)
  waiting for transfers between devices: 28.3 us -> 34.4 us
  Pallas kernels: 17.9 us -> 15.6 us
  local copies, waits for them, and re-layouts: 3.94 us -> 1.99 us
    ppermute x15 -> x16, waiting for transfers between devices: 21.8 us -> 27.9 us  [flip(): return lax.ppermute(x, 'ctx', [(i, i ^ bit) for i in range(ctx_size)])]
    pallas_call x1, Pallas kernels: 7.46 us -> 4.43 us  [body(): pl.pallas_call(video_kernel, grid=(steps,), compiler_params=PARAMS, in_sp...]
    unnamed x20 -> x14, local copies, waits for them, and re-layouts: 3.9 us -> 1.94 us
    pallas_call x3 -> x6, Pallas kernels: 1.59 us -> 3.23 us  [the longest x1 1.43 us: body(): pl.pallas_call(pack_kernel, in_specs=[pl.BlockSpec(memory_space=pltpu.HBM...]
    ppermute x15 -> x16, starting transfers between devices: 19.3 us -> 19.9 us  [flip(): return lax.ppermute(x, 'ctx', [(i, i ^ bit) for i in range(ctx_size)])]
  transfers between devices with their start and end apart: 17 -> 18, of which waited for: 11 -> 14; matrix products, arithmetic and copies ran while one was open for 1% -> 3% of each run, Pallas kernels for 17% -> 12%
where the time goes in v3:
time: 77.8 us; the launch traced here: 77.4 us
  waiting for transfers between devices  34.4 us (44%)
  starting transfers between devices  23 us (30%)
  Pallas kernels  15.6 us (20%)
  local copies, waits for them, and re-layouts  1.99 us (3%)
  between operations  1.5 us (2%)
  other arithmetic  1.04 us (1%)
    ppermute x16, waiting for transfers between devices, flip(): return lax.ppermute(x, 'ctx', [(i, i ^ bit) for i in range(ctx_size)])  27.9 us
    ppermute x16, starting transfers between devices, flip(): return lax.ppermute(x, 'ctx', [(i, i ^ bit) for i in range(ctx_size)])  19.9 us
    ppermute x1, waiting for transfers between devices, body(): got = lax.ppermute(sent, 'head', [(0, 1), (1, 0)])  6.48 us
    pallas_call x1, Pallas kernels, body(): pl.pallas_call(video_kernel, grid=(steps,), compiler_params=PARAMS, in_sp...  4.43 us
    pallas_call x1, Pallas kernels, body(): pl.pallas_call(audio_kernel, grid=(steps,), compiler_params=PARAMS, in_sp...  3.82 us
    pallas_call x1, Pallas kernels, body(): pl.pallas_call(final_kernel, grid=(steps,), compiler_params=PARAMS, in_sp...  3.23 us
    unnamed x14, local copies, waits for them, and re-layouts  1.94 us
    ppermute x1, starting transfers between devices, body(): got = lax.ppermute(sent, 'head', [(0, 1), (1, 0)])  1.58 us
  transfers between devices with their start and end apart: 18, of which 14 were waited for; matrix products, arithmetic and copies ran while one was open for 3% of the time, Pallas kernels for 12%

profile of v3, /device:TPU:0, one launch (start us, length us, event | category | flops | bytes accessed | tf_op | source)
XLA Modules:
  0.0 77.4 jit_solution(15496533360213007424)
XLA Ops:
  0.6 1.4 %pack.1 = bf16[8,4096]{1,0:T(8,128)(2,1)} custom-call(bf16[8,1024]{1,0:T(8,128)(2,1)} %refs_0_.1, bf16[8,1024]{1,0:T(8,128)(2,1)} %refs_1_.1, bf16[8,1024]{1,0:T(8,128)(2,1)} %refs_2_.1, bf16[8,1024]{1,0:T(8,128)(2,1)} %refs_3_.1), custom_call_target="tpu_custom_call" | custom-call | tf_op jit(solution)/shard_map/pack/pallas_call | solution.py:302
  2.1 0.0 copy-start.3
  2.1 4.1 %collective-permute-start = (bf16[8,4096]{1,0:T(8,128)(2,1)}, bf16[8,4096]{1,0:T(8,128)(2,1)S(1)}, u32[]{:S(2)}, u32[]{:S(2)}) collective-permute-start(bf16[8,4096]{1,0:T(8,128)(2,1)} %pack.1), channel_id=1, source_target_pairs={{0,8},{1,9},{2,10},{3,11},{4,12},{5,13},{6,14},{7,15},{8,0},{9,1},... | collective-permute-start | bytes 196616 | tf_op jit(solution)/shard_map/ppermute | solution.py:286
  6.2 1.6 %collective-permute-start.1 = (bf16[8,4096]{1,0:T(8,128)(2,1)}, bf16[8,4096]{1,0:T(8,128)(2,1)S(1)}, u32[]{:S(2)}, u32[]{:S(2)}) collective-permute-start(bf16[8,4096]{1,0:T(8,128)(2,1)} %pack.1), channel_id=1, source_target_pairs={{0,4},{1,5},{2,6},{3,7},{4,0},{5,1},{6,2},{7,3},{8,12},{9,13},{10,... | collective-permute-start | bytes 196616 | tf_op jit(solution)/shard_map/ppermute | solution.py:286
  7.8 0.9 %constant_dynamic-update-slice_fusion.4 = bf16[64,4096]{1,0:T(8,128)(2,1)S(1)} fusion(bf16[8,4096]{1,0:T(8,128)(2,1)} %pack.1), kind=kLoop, calls=%fused_computation.12 | loop fusion | bytes 131072
  8.7 0.8 collective-permute-done
  9.5 1.2 %collective-permute-done.1 = bf16[8,4096]{1,0:T(8,128)(2,1)S(1)} collective-permute-done((bf16[8,4096]{1,0:T(8,128)(2,1)}, bf16[8,4096]{1,0:T(8,128)(2,1)S(1)}, u32[]{:S(2)}, u32[]{:S(2)}) %collective-permute-start.1) | collective-permute-done | bytes 65568 | tf_op jit(solution)/shard_map/ppermute | solution.py:286
  10.7 3.4 %collective-permute-done.2 = bf16[8,4096]{1,0:T(8,128)(2,1)S(1)} collective-permute-done((bf16[8,4096]{1,0:T(8,128)(2,1)}, bf16[8,4096]{1,0:T(8,128)(2,1)S(1)}, u32[]{:S(2)}, u32[]{:S(2)}) %collective-permute-start.2) | collective-permute-done | bytes 65568 | tf_op jit(solution)/shard_map/ppermute | solution.py:286
  14.1 0.0 copy-start.4
  14.1 1.6 %collective-permute-start.3 = (bf16[32,4096]{1,0:T(8,128)(2,1)S(1)}, bf16[32,4096]{1,0:T(8,128)(2,1)S(1)}, u32[]{:S(2)}, u32[]{:S(2)}) collective-permute-start(bf16[32,4096]{1,0:T(8,128)(2,1)S(1)} %pad_maximum_fusion.1), channel_id=1, source_target_pairs={{0,2},{1,3},{2,0},{3,1},{4,6},{5,7},{6,4},{7,5},{8,10},{9,11},{10,... | collective-permute-start | bytes 786440 | tf_op jit(solution)/shard_map/ppermute | solution.py:286
  15.7 4.9 %collective-permute-done.3 = bf16[32,4096]{1,0:T(8,128)(2,1)S(1)} collective-permute-done((bf16[32,4096]{1,0:T(8,128)(2,1)S(1)}, bf16[32,4096]{1,0:T(8,128)(2,1)S(1)}, u32[]{:S(2)}, u32[]{:S(2)}) %collective-permute-start.3) | collective-permute-done | bytes 262176 | tf_op jit(solution)/shard_map/ppermute | solution.py:286
  20.6 0.1 collective-permute-start.4
  20.8 1.6 %collective-permute-start.5 = (bf16[128,1024]{1,0:T(8,128)(2,1)S(1)}, bf16[128,1024]{1,0:T(8,128)(2,1)S(1)}, u32[]{:S(2)}, u32[]{:S(2)}) collective-permute-start(bf16[128,1024]{1,0:T(8,128)(2,1)S(1)} %dynamic-slice_bitcast_fusion), channel_id=1, source_target_pairs={{0,16},{16,0},{1,17},{17,1},{2,18},{18,2},{3,19},{19,3},{4,20},{20... | collective-permute-start | bytes 786440 | tf_op jit(solution)/shard_map/ppermute | solution.py:295
  23.0 0.0 copy-start
  23.0 0.0 copy-start.1
  23.0 6.5 %collective-permute-done.5 = bf16[128,1024]{1,0:T(8,128)(2,1)S(1)} collective-permute-done((bf16[128,1024]{1,0:T(8,128)(2,1)S(1)}, bf16[128,1024]{1,0:T(8,128)(2,1)S(1)}, u32[]{:S(2)}, u32[]{:S(2)}) %collective-permute-start.5) | collective-permute-done | bytes 262176 | tf_op jit(solution)/shard_map/ppermute | solution.py:295
  29.5 0.1 bitcast_select_fusion.1
  29.7 3.8 %audio_side.1 = (f32[8,8,128]{2,1,0:T(8,128)S(1)}, f32[3,64,1024]{2,1,0:T(8,128)S(1)}, bf16[3,64,1024]{2,1,0:T(8,128)(2,1)S(1)}) custom-call(s32[1]{0:T(128)S(6)} %min.6.live_ref, bf16[64,4096]{1,0:T(8,128)(2,1)S(1)} %constant_dynamic-update-slice_fusion.k_lo.v_lo.q_lo.c_lo, bf16[64,4096]{1,0:T(8,128)(2,1)S(1)} %collective-permute-done.4.k_hi.v_hi.q_hi.c_hi, ...), custom_call_target="tpu_custom_call" | custom-call | flops 671088640 | bytes 2621440 | tf_op jit(solution)/shard_map/audio_side/pallas_call | solution.py:344
  33.5 0.1 collective-permute-start.11
  33.6 1.0 %copy-done.2 = bf16[256,1024]{1,0:T(8,128)(2,1)S(1)} copy-done((bf16[256,1024]{1,0:T(8,128)(2,1)S(1)}, bf16[256,1024]{1,0:T(8,128)(2,1)}, u32[]{:S(2)}) %copy-start.2) | copy-done | bytes 524312
  34.6 4.4 %video_side.1 = (bf16[128,1024]{1,0:T(8,128)(2,1)S(1)}, bf16[128,1024]{1,0:T(8,128)(2,1)S(1)}, bf16[256,1024]{1,0:T(8,128)(2,1)}, f32[2,64,1024]{2,1,0:T(8,128)S(1)}, bf16[2,64,1024]{2,1,0:T(8,128)(2,1)S(1)}) custom-call(s32[1]{0:T(128)} %bitcast.head_ref, bf16[64,4096]{1,0:T(8,128)(2,1)S(1)} %constant_dynamic-update-slice_fusion.k_lo.v_lo.q_lo.c_lo, ...), custom_call_target="tpu_custom_call" | custom-call | flops 805306368 | bytes 3145728 | tf_op jit(solution)/shard_map/video_side/pallas_call | solution.py:361
  39.0 0.5 collective-permute-start.13
  39.5 1.5 %collective-permute-start.6 = (bf16[128,1024]{1,0:T(8,128)(2,1)S(1)}, bf16[128,1024]{1,0:T(8,128)(2,1)S(1)}, u32[]{:S(2)}, u32[]{:S(2)}) collective-permute-start(bf16[128,1024]{1,0:T(8,128)(2,1)S(1)} %get-tuple-element.31), channel_id=1, source_target_pairs={{0,16},{16,0},{1,17},{17,1},{2,18},{18,2},{3,19},{19,3},{4,20},{20... | collective-permute-start | bytes 786440 | tf_op jit(solution)/shard_map/ppermute | solution.py:374
  41.1 1.2 %collective-permute-done.7.other_ref = f32[8,8,128]{2,1,0:T(8,128)S(1)} collective-permute-done((f32[8,8,128]{2,1,0:T(8,128)S(1)}, f32[8,8,128]{2,1,0:T(8,128)S(1)}, u32[]{:S(2)}, u32[]{:S(2)}) %collective-permute-start.7) | collective-permute-done | bytes 32800 | tf_op jit(solution)/shard_map/ppermute | solution.py:286
  42.3 0.1 shard_map.152.mine_ref
  42.4 1.6 %collective-permute-start.8 = (f32[8,8,128]{2,1,0:T(8,128)S(1)}, f32[8,8,128]{2,1,0:T(8,128)S(1)}, u32[]{:S(2)}, u32[]{:S(2)}) collective-permute-start(f32[8,8,128]{2,1,0:T(8,128)S(1)} %shard_map.152.mine_ref), channel_id=1, source_target_pairs={{0,2},{1,3},{2,0},{3,1},{4,6},{5,7},{6,4},{7,5},{8,10},{9,11},{10,... | collective-permute-start | bytes 98312 | tf_op jit(solution)/shard_map/ppermute | solution.py:286
  43.9 2.4 %collective-permute-done.8.other_ref = f32[8,8,128]{2,1,0:T(8,128)S(1)} collective-permute-done((f32[8,8,128]{2,1,0:T(8,128)S(1)}, f32[8,8,128]{2,1,0:T(8,128)S(1)}, u32[]{:S(2)}, u32[]{:S(2)}) %collective-permute-start.8) | collective-permute-done | bytes 32800 | tf_op jit(solution)/shard_map/ppermute | solution.py:286
  46.3 0.1 shard_map.153.mine_ref
  46.5 0.9 %collective-permute-start.9 = (f32[8,8,128]{2,1,0:T(8,128)S(1)}, f32[8,8,128]{2,1,0:T(8,128)S(1)}, u32[]{:S(2)}, u32[]{:S(2)}) collective-permute-start(f32[8,8,128]{2,1,0:T(8,128)S(1)} %shard_map.153.mine_ref), channel_id=1, source_target_pairs={{0,4},{1,5},{2,6},{3,7},{4,0},{5,1},{6,2},{7,3},{8,12},{9,13},{10,... | collective-permute-start | bytes 98312 | tf_op jit(solution)/shard_map/ppermute | solution.py:286
  47.3 3.1 %collective-permute-done.9.other_ref = f32[8,8,128]{2,1,0:T(8,128)S(1)} collective-permute-done((f32[8,8,128]{2,1,0:T(8,128)S(1)}, f32[8,8,128]{2,1,0:T(8,128)S(1)}, u32[]{:S(2)}, u32[]{:S(2)}) %collective-permute-start.9) | collective-permute-done | bytes 32800 | tf_op jit(solution)/shard_map/ppermute | solution.py:286
  50.4 0.1 shard_map.154.mine_ref
  50.6 2.9 %collective-permute-start.10 = (f32[8,8,128]{2,1,0:T(8,128)S(1)}, f32[8,8,128]{2,1,0:T(8,128)S(1)}, u32[]{:S(2)}, u32[]{:S(2)}) collective-permute-start(f32[8,8,128]{2,1,0:T(8,128)S(1)} %shard_map.154.mine_ref), channel_id=1, source_target_pairs={{0,8},{1,9},{2,10},{3,11},{4,12},{5,13},{6,14},{7,15},{8,0},{9,1},... | collective-permute-start | bytes 98312 | tf_op jit(solution)/shard_map/ppermute | solution.py:286
  53.5 1.9 %collective-permute-done.10.other_ref = f32[8,8,128]{2,1,0:T(8,128)S(1)} collective-permute-done((f32[8,8,128]{2,1,0:T(8,128)S(1)}, f32[8,8,128]{2,1,0:T(8,128)S(1)}, u32[]{:S(2)}, u32[]{:S(2)}) %collective-permute-start.10) | collective-permute-done | bytes 32800 | tf_op jit(solution)/shard_map/ppermute | solution.py:286
  55.4 0.1 shard_map.155.all_ref.stat_ref
  55.6 3.2 %audio_grads.1 = (bf16[256,1024]{1,0:T(8,128)(2,1)}, bf16[256,1024]{1,0:T(8,128)(2,1)}) custom-call(s32[1]{0:T(128)S(6)} %min.6.live_ref, bf16[64,4096]{1,0:T(8,128)(2,1)S(1)} %constant_dynamic-update-slice_fusion.k_lo.v_lo.q_lo.c_lo, bf16[64,4096]{1,0:T(8,128)(2,1)S(1)} %collective-permute-done.4.k_hi.v_hi.q_hi.c_hi, ...), custom_call_target="tpu_custom_call" | custom-call | flops 536870912 | bytes 2097152 | tf_op jit(solution)/shard_map/audio_grads/pallas_call | solution.py:425
  58.8 1.9 %collective-permute-start.14 = (bf16[2,32,1024]{2,1,0:T(8,128)(2,1)S(1)}, bf16[2,32,1024]{2,1,0:T(8,128)(2,1)S(1)}, u32[]{:S(2)}, u32[]{:S(2)}) collective-permute-start(bf16[2,32,1024]{2,1,0:T(8,128)(2,1)S(1)} %get-tuple-element.40), channel_id=1, source_target_pairs={{0,2},{1,3},{2,0},{3,1},{4,6},{5,7},{6,4},{7,5},{8,10},{9,11},{10,... | collective-permute-start | bytes 393224 | tf_op jit(solution)/shard_map/ppermute | solution.py:286
  60.7 0.9 %shard_map.156 = (f32[3,32,1024]{2,1,0:T(8,128)S(1)}, bf16[3,32,1024]{2,1,0:T(8,128)(2,1)S(1)}) custom-call(f32[8,8,128]{2,1,0:T(8,128)S(1)} %get-tuple-element.32.mine_ref, f32[8,8,128]{2,1,0:T(8,128)S(1)} %collective-permute-done.7.other_ref, f32[3,64,1024]{2,1,0:T(8,128)S(1)} %get-tuple-element.33.keep, bf16[3,64,1024]{2,1,0:T(8,128)(2,1)S(1)} %collective-permute-done.11.recv), custom_call_target="tpu_custom_call" | custom-call | tf_op jit(solution)/shard_map/pallas_call | solution.py:392
  61.7 0.3 collective-permute-start.12
  62.0 2.7 %collective-permute-done.14.recv_b = bf16[2,32,1024]{2,1,0:T(8,128)(2,1)S(1)} collective-permute-done((bf16[2,32,1024]{2,1,0:T(8,128)(2,1)S(1)}, bf16[2,32,1024]{2,1,0:T(8,128)(2,1)S(1)}, u32[]{:S(2)}, u32[]{:S(2)}) %collective-permute-start.14) | collective-permute-done | bytes 131104 | tf_op jit(solution)/shard_map/ppermute | solution.py:286
  64.7 2.7 %collective-permute-done.12.recv_a = bf16[3,32,1024]{2,1,0:T(8,128)(2,1)S(1)} collective-permute-done((bf16[3,32,1024]{2,1,0:T(8,128)(2,1)S(1)}, bf16[3,32,1024]{2,1,0:T(8,128)(2,1)S(1)}, u32[]{:S(2)}, u32[]{:S(2)}) %collective-permute-start.12) | collective-permute-done | bytes 196640 | tf_op jit(solution)/shard_map/ppermute | solution.py:286
  67.4 0.6 settle.1
  68.0 2.6 %collective-permute-start.15 = (bf16[4,8,1024]{2,1,0:T(8,128)(2,1)S(1)}, bf16[4,8,1024]{2,1,0:T(8,128)(2,1)S(1)}, u32[]{:S(2)}, u32[]{:S(2)}) collective-permute-start(bf16[4,8,1024]{2,1,0:T(8,128)(2,1)S(1)} %get-tuple-element.42), channel_id=1, source_target_pairs={{0,8},{1,9},{2,10},{3,11},{4,12},{5,13},{6,14},{7,15},{8,0},{9,1},... | collective-permute-start | bytes 196616 | tf_op jit(solution)/shard_map/ppermute | solution.py:286
  70.6 1.8 %collective-permute-start.17 = (bf16[4,8,1024]{2,1,0:T(8,128)(2,1)S(1)}, bf16[4,8,1024]{2,1,0:T(8,128)(2,1)S(1)}, u32[]{:S(2)}, u32[]{:S(2)}) collective-permute-start(bf16[4,8,1024]{2,1,0:T(8,128)(2,1)S(1)} %get-tuple-element.44), channel_id=1, source_target_pairs={{0,12},{1,13},{2,14},{3,15},{4,8},{5,9},{6,10},{7,11},{8,4},{9,5},... | collective-permute-start | bytes 196616 | tf_op jit(solution)/shard_map/ppermute | solution.py:286
  72.5 0.8 %maximum_bitcast_fusion = bf16[1,128,2048]{2,1,0:T(8,128)(2,1)} fusion(bf16[128,1024]{1,0:T(8,128)(2,1)S(1)} %get-tuple-element.55, bf16[128,1024]{1,0:T(8,128)(2,1)S(1)} %get-tuple-element.54), kind=kLoop, calls=%fused_computation.1 | loop fusion | flops 1048576 | bytes 1048576 | tf_op jit(solution)/shard_map/broadcast_in_dim | solution.py:375
  73.3 0.6 collective-permute-done.15.refs_1_
  73.9 0.9 %collective-permute-done.16.refs_2_ = bf16[4,8,1024]{2,1,0:T(8,128)(2,1)S(1)} collective-permute-done((bf16[4,8,1024]{2,1,0:T(8,128)(2,1)S(1)}, bf16[4,8,1024]{2,1,0:T(8,128)(2,1)S(1)}, u32[]{:S(2)}, u32[]{:S(2)}) %collective-permute-start.16) | collective-permute-done | bytes 65568 | tf_op jit(solution)/shard_map/ppermute | solution.py:286
  74.9 1.9 %collective-permute-done.17.refs_3_ = bf16[4,8,1024]{2,1,0:T(8,128)(2,1)S(1)} collective-permute-done((bf16[4,8,1024]{2,1,0:T(8,128)(2,1)S(1)}, bf16[4,8,1024]{2,1,0:T(8,128)(2,1)S(1)}, u32[]{:S(2)}, u32[]{:S(2)}) %collective-permute-start.17) | collective-permute-done | bytes 65568 | tf_op jit(solution)/shard_map/ppermute | solution.py:286
  76.8 0.6 add.9
  (21 shorter events, 0.2 us)
Async XLA Ops:
  2.1 12.0 %copy-start.3 = (bf16[8,4096]{1,0:T(8,128)(2,1)S(1)}, bf16[8,4096]{1,0:T(8,128)(2,1)}, u32[]{:S(2)}) copy-start(bf16[8,4096]{1,0:T(8,128)(2,1)} %pack.1) | copy-start | bytes 196612
  2.1 7.4 %collective-permute-start = (bf16[8,4096]{1,0:T(8,128)(2,1)}, bf16[8,4096]{1,0:T(8,128)(2,1)S(1)}, u32[]{:S(2)}, u32[]{:S(2)}) collective-permute-start(bf16[8,4096]{1,0:T(8,128)(2,1)} %pack.1), channel_id=1, source_target_pairs={{0,8},{1,9},{2,10},{3,11},{4,12},{5,13},{6,14},{7,15},{8,0},{9,1},... | collective-permute-start | bytes 196616 | tf_op jit(solution)/shard_map/ppermute | solution.py:286
  6.2 4.5 %collective-permute-start.1 = (bf16[8,4096]{1,0:T(8,128)(2,1)}, bf16[8,4096]{1,0:T(8,128)(2,1)S(1)}, u32[]{:S(2)}, u32[]{:S(2)}) collective-permute-start(bf16[8,4096]{1,0:T(8,128)(2,1)} %pack.1), channel_id=1, source_target_pairs={{0,4},{1,5},{2,6},{3,7},{4,0},{5,1},{6,2},{7,3},{8,12},{9,13},{10,... | collective-permute-start | bytes 196616 | tf_op jit(solution)/shard_map/ppermute | solution.py:286
  7.8 6.3 %collective-permute-start.2 = (bf16[8,4096]{1,0:T(8,128)(2,1)}, bf16[8,4096]{1,0:T(8,128)(2,1)S(1)}, u32[]{:S(2)}, u32[]{:S(2)}) collective-permute-start(bf16[8,4096]{1,0:T(8,128)(2,1)} %pack.1), channel_id=1, source_target_pairs={{0,12},{1,13},{2,14},{3,15},{4,8},{5,9},{6,10},{7,11},{8,4},{9,5},... | collective-permute-start | bytes 196616 | tf_op jit(solution)/shard_map/ppermute | solution.py:286
  14.1 6.6 %copy-start.4 = (bf16[1,128,2048]{2,1,0:T(8,128)(2,1)S(1)}, bf16[1,128,2048]{2,1,0:T(8,128)(2,1)}, u32[]{:S(2)}) copy-start(bf16[1,128,2048]{2,1,0:T(8,128)(2,1)} %param.16) | copy-start | bytes 1572868
  14.1 6.5 %collective-permute-start.3 = (bf16[32,4096]{1,0:T(8,128)(2,1)S(1)}, bf16[32,4096]{1,0:T(8,128)(2,1)S(1)}, u32[]{:S(2)}, u32[]{:S(2)}) collective-permute-start(bf16[32,4096]{1,0:T(8,128)(2,1)S(1)} %pad_maximum_fusion.1), channel_id=1, source_target_pairs={{0,2},{1,3},{2,0},{3,1},{4,6},{5,7},{6,4},{7,5},{8,10},{9,11},{10,... | collective-permute-start | bytes 786440 | tf_op jit(solution)/shard_map/ppermute | solution.py:286
  20.6 9.0 %collective-permute-start.4 = (bf16[64,4096]{1,0:T(8,128)(2,1)S(1)}, bf16[64,4096]{1,0:T(8,128)(2,1)S(1)}, u32[]{:S(2)}, u32[]{:S(2)}) collective-permute-start(bf16[64,4096]{1,0:T(8,128)(2,1)S(1)} %constant_dynamic-update-slice_fusion.k_lo.v_lo.q_lo.c_lo), channel_id=1, source_target_pairs={{0,1},{1,0},{2,3},{3,2},{4,5},{5,4},{6,7},{7,6},{8,9},{9,8},{10,11... | collective-permute-start | bytes 1572872 | tf_op jit(solution)/shard_map/ppermute | solution.py:286
  20.8 8.8 %collective-permute-start.5 = (bf16[128,1024]{1,0:T(8,128)(2,1)S(1)}, bf16[128,1024]{1,0:T(8,128)(2,1)S(1)}, u32[]{:S(2)}, u32[]{:S(2)}) collective-permute-start(bf16[128,1024]{1,0:T(8,128)(2,1)S(1)} %dynamic-slice_bitcast_fusion), channel_id=1, source_target_pairs={{0,16},{16,0},{1,17},{17,1},{2,18},{18,2},{3,19},{19,3},{4,20},{20... | collective-permute-start | bytes 786440 | tf_op jit(solution)/shard_map/ppermute | solution.py:295
  23.0 6.6 %copy-start = (bf16[256,1024]{1,0:T(8,128)(2,1)S(1)}, bf16[256,1024]{1,0:T(8,128)(2,1)}, u32[]{:S(2)}) copy-start(bf16[256,1024]{1,0:T(8,128)(2,1)} %key_ref.3) | copy-start | bytes 1572868
  23.0 6.6 %copy-start.1 = (bf16[256,1024]{1,0:T(8,128)(2,1)S(1)}, bf16[256,1024]{1,0:T(8,128)(2,1)}, u32[]{:S(2)}) copy-start(bf16[256,1024]{1,0:T(8,128)(2,1)} %val_ref.3) | copy-start | bytes 1572868
  33.5 27.2 %collective-permute-start.11 = (bf16[3,64,1024]{2,1,0:T(8,128)(2,1)S(1)}, bf16[3,64,1024]{2,1,0:T(8,128)(2,1)S(1)}, u32[]{:S(2)}, u32[]{:S(2)}) collective-permute-start(bf16[3,64,1024]{2,1,0:T(8,128)(2,1)S(1)} %get-tuple-element.34), channel_id=1, source_target_pairs={{0,1},{1,0},{2,3},{3,2},{4,5},{5,4},{6,7},{7,6},{8,9},{9,8},{10,11... | collective-permute-start | bytes 1179656 | tf_op jit(solution)/shard_map/ppermute | solution.py:286
  33.6 1.0 %copy-start.2 = (bf16[256,1024]{1,0:T(8,128)(2,1)S(1)}, bf16[256,1024]{1,0:T(8,128)(2,1)}, u32[]{:S(2)}) copy-start(bf16[256,1024]{1,0:T(8,128)(2,1)} %query_ref.1) | copy-start | bytes 1572868
  39.0 19.7 %collective-permute-start.13 = (bf16[2,64,1024]{2,1,0:T(8,128)(2,1)S(1)}, bf16[2,64,1024]{2,1,0:T(8,128)(2,1)S(1)}, u32[]{:S(2)}, u32[]{:S(2)}) collective-permute-start(bf16[2,64,1024]{2,1,0:T(8,128)(2,1)S(1)} %get-tuple-element.38), channel_id=1, source_target_pairs={{0,1},{1,0},{2,3},{3,2},{4,5},{5,4},{6,7},{7,6},{8,9},{9,8},{10,11... | collective-permute-start | bytes 786440 | tf_op jit(solution)/shard_map/ppermute | solution.py:286
  39.5 22.4 %collective-permute-start.6 = (bf16[128,1024]{1,0:T(8,128)(2,1)S(1)}, bf16[128,1024]{1,0:T(8,128)(2,1)S(1)}, u32[]{:S(2)}, u32[]{:S(2)}) collective-permute-start(bf16[128,1024]{1,0:T(8,128)(2,1)S(1)} %get-tuple-element.31), channel_id=1, source_target_pairs={{0,16},{16,0},{1,17},{17,1},{2,18},{18,2},{3,19},{19,3},{4,20},{20... | collective-permute-start | bytes 786440 | tf_op jit(solution)/shard_map/ppermute | solution.py:374
  41.1 1.2 %collective-permute-start.7 = (f32[8,8,128]{2,1,0:T(8,128)S(1)}, f32[8,8,128]{2,1,0:T(8,128)S(1)}, u32[]{:S(2)}, u32[]{:S(2)}) collective-permute-start(f32[8,8,128]{2,1,0:T(8,128)S(1)} %get-tuple-element.32.mine_ref), channel_id=1, source_target_pairs={{0,1},{1,0},{2,3},{3,2},{4,5},{5,4},{6,7},{7,6},{8,9},{9,8},{10,11... | collective-permute-start | bytes 98312 | tf_op jit(solution)/shard_map/ppermute | solution.py:286
  42.4 4.0 %collective-permute-start.8 = (f32[8,8,128]{2,1,0:T(8,128)S(1)}, f32[8,8,128]{2,1,0:T(8,128)S(1)}, u32[]{:S(2)}, u32[]{:S(2)}) collective-permute-start(f32[8,8,128]{2,1,0:T(8,128)S(1)} %shard_map.152.mine_ref), channel_id=1, source_target_pairs={{0,2},{1,3},{2,0},{3,1},{4,6},{5,7},{6,4},{7,5},{8,10},{9,11},{10,... | collective-permute-start | bytes 98312 | tf_op jit(solution)/shard_map/ppermute | solution.py:286
  46.5 4.0 %collective-permute-start.9 = (f32[8,8,128]{2,1,0:T(8,128)S(1)}, f32[8,8,128]{2,1,0:T(8,128)S(1)}, u32[]{:S(2)}, u32[]{:S(2)}) collective-permute-start(f32[8,8,128]{2,1,0:T(8,128)S(1)} %shard_map.153.mine_ref), channel_id=1, source_target_pairs={{0,4},{1,5},{2,6},{3,7},{4,0},{5,1},{6,2},{7,3},{8,12},{9,13},{10,... | collective-permute-start | bytes 98312 | tf_op jit(solution)/shard_map/ppermute | solution.py:286
  50.6 4.9 %collective-permute-start.10 = (f32[8,8,128]{2,1,0:T(8,128)S(1)}, f32[8,8,128]{2,1,0:T(8,128)S(1)}, u32[]{:S(2)}, u32[]{:S(2)}) collective-permute-start(f32[8,8,128]{2,1,0:T(8,128)S(1)} %shard_map.154.mine_ref), channel_id=1, source_target_pairs={{0,8},{1,9},{2,10},{3,11},{4,12},{5,13},{6,14},{7,15},{8,0},{9,1},... | collective-permute-start | bytes 98312 | tf_op jit(solution)/shard_map/ppermute | solution.py:286
  58.8 5.9 %collective-permute-start.14 = (bf16[2,32,1024]{2,1,0:T(8,128)(2,1)S(1)}, bf16[2,32,1024]{2,1,0:T(8,128)(2,1)S(1)}, u32[]{:S(2)}, u32[]{:S(2)}) collective-permute-start(bf16[2,32,1024]{2,1,0:T(8,128)(2,1)S(1)} %get-tuple-element.40), channel_id=1, source_target_pairs={{0,2},{1,3},{2,0},{3,1},{4,6},{5,7},{6,4},{7,5},{8,10},{9,11},{10,... | collective-permute-start | bytes 393224 | tf_op jit(solution)/shard_map/ppermute | solution.py:286
  61.7 5.7 %collective-permute-start.12 = (bf16[3,32,1024]{2,1,0:T(8,128)(2,1)S(1)}, bf16[3,32,1024]{2,1,0:T(8,128)(2,1)S(1)}, u32[]{:S(2)}, u32[]{:S(2)}) collective-permute-start(bf16[3,32,1024]{2,1,0:T(8,128)(2,1)S(1)} %get-tuple-element.36), channel_id=1, source_target_pairs={{0,2},{1,3},{2,0},{3,1},{4,6},{5,7},{6,4},{7,5},{8,10},{9,11},{10,... | collective-permute-start | bytes 589832 | tf_op jit(solution)/shard_map/ppermute | solution.py:286
  68.0 5.9 %collective-permute-start.15 = (bf16[4,8,1024]{2,1,0:T(8,128)(2,1)S(1)}, bf16[4,8,1024]{2,1,0:T(8,128)(2,1)S(1)}, u32[]{:S(2)}, u32[]{:S(2)}) collective-permute-start(bf16[4,8,1024]{2,1,0:T(8,128)(2,1)S(1)} %get-tuple-element.42), channel_id=1, source_target_pairs={{0,8},{1,9},{2,10},{3,11},{4,12},{5,13},{6,14},{7,15},{8,0},{9,1},... | collective-permute-start | bytes 196616 | tf_op jit(solution)/shard_map/ppermute | solution.py:286
  70.6 4.3 %collective-permute-start.16 = (bf16[4,8,1024]{2,1,0:T(8,128)(2,1)S(1)}, bf16[4,8,1024]{2,1,0:T(8,128)(2,1)S(1)}, u32[]{:S(2)}, u32[]{:S(2)}) collective-permute-start(bf16[4,8,1024]{2,1,0:T(8,128)(2,1)S(1)} %get-tuple-element.43), channel_id=1, source_target_pairs={{0,4},{1,5},{2,6},{3,7},{4,0},{5,1},{6,2},{7,3},{8,12},{9,13},{10,... | collective-permute-start | bytes 196616 | tf_op jit(solution)/shard_map/ppermute | solution.py:286
  70.6 6.2 %collective-permute-start.17 = (bf16[4,8,1024]{2,1,0:T(8,128)(2,1)S(1)}, bf16[4,8,1024]{2,1,0:T(8,128)(2,1)S(1)}, u32[]{:S(2)}, u32[]{:S(2)}) collective-permute-start(bf16[4,8,1024]{2,1,0:T(8,128)(2,1)S(1)} %get-tuple-element.44), channel_id=1, source_target_pairs={{0,12},{1,13},{2,14},{3,15},{4,8},{5,9},{6,10},{7,11},{8,4},{9,5},... | collective-permute-start | bytes 196616 | tf_op jit(solution)/shard_map/ppermute | solution.py:286
